TPU v7x, 128 devices: a whole 4x4x4 slice. The times are simulated.
128 devices in a mesh: tp: 2 (over core), fsdp: 64 (over z, y, x).
Axes of the slice: x: 4, y: 4, z: 4, core: 2. Of those that a mesh axis runs over, the one named last changes fastest.
Arguments:
- resid_in: bfloat16 [64, 1536, 1536], P('fsdp', 'tp')
- grad_out: bfloat16 [64, 1536, 1536], P('fsdp', 'tp')
- norm_gain: float32 [1536], replicated
- w_qkv: bfloat16 [1536, 2048], P('fsdp', 'tp')
- b_qkv: bfloat16 [2048], P('tp')
- sinks: float32 [12], P('tp')
- w_out: bfloat16 [1536, 1536], P(('tp', 'fsdp'))
- b_out: bfloat16 [1536], replicated
Outputs:
- output 1: bfloat16 [64, 1536, 1536], P('fsdp', 'tp')
- output 2: bfloat16 [64, 1536, 1536], P('fsdp', 'tp')
- output 3: float32 [1536], replicated
- output 4: float32 [1536, 2048], P('fsdp', 'tp')
- output 5: float32 [2048], P('tp')
- output 6: float32 [12], P('tp')
- output 7: float32 [1536, 1536], P(('tp', 'fsdp'))
- output 8: float32 [1536], replicated
All inputs are finite; a program needn't handle non-finite values.
Results may differ from a plain program's by a relative error of at most 0.0108284.
Values are sent between devices in bfloat16 or wider.
A program may use at most 1 GiB of HBM per device.

v0:
```python
import jax
import jax.numpy as jnp
from jax import lax
from jax.sharding import PartitionSpec as P

EPS = 1e-5
ROPE_BASE = 150000.0
WINDOW = 128


def rope_tables(positions, head_dim):
    inv_freq = ROPE_BASE ** (-2.0 * jnp.arange(head_dim // 2).astype(jnp.float32) / head_dim)
    angles = positions.astype(jnp.float32)[:, None] * inv_freq[None, :]
    return jnp.cos(angles), jnp.sin(angles)


def apply_rope(head_vals, cos_tab, sin_tab):
    half_dim = head_vals.shape[-1] // 2
    first_half = head_vals[..., :half_dim]
    second_half = head_vals[..., half_dim:]
    return jnp.concatenate([first_half * cos_tab - second_half * sin_tab, second_half * cos_tab + first_half * sin_tab], axis=-1)


def rope_back(head_grads, cos_tab, sin_tab):
    half_dim = head_grads.shape[-1] // 2
    first_half = head_grads[..., :half_dim]
    second_half = head_grads[..., half_dim:]
    return jnp.concatenate([first_half * cos_tab + second_half * sin_tab, second_half * cos_tab - first_half * sin_tab], axis=-1)


def split_qkv(qkv_proj, positions, kv_count, head_dim):
    n_rows, seq_len = qkv_proj.shape[0], qkv_proj.shape[1]
    grouped = qkv_proj.reshape(n_rows, seq_len, kv_count, -1, head_dim)
    group_size = grouped.shape[3] - 2
    cos_tab, sin_tab = rope_tables(positions, head_dim)
    queries = apply_rope(grouped[:, :, :, :group_size].astype(jnp.float32), cos_tab[:, None, None], sin_tab[:, None, None])
    keys_rot = apply_rope(grouped[:, :, :, group_size].astype(jnp.float32), cos_tab[:, None], sin_tab[:, None])
    return queries.astype(jnp.bfloat16), keys_rot.astype(jnp.bfloat16), grouped[:, :, :, group_size + 1]


def band_mask(first_pos, blk_start):
    q_idx = jnp.arange(WINDOW)[:, None]
    k_idx = jnp.arange(2 * WINDOW)[None, :]
    return (k_idx > q_idx) & (k_idx <= q_idx + WINDOW) & (first_pos + blk_start - WINDOW + k_idx >= 0)


def block_scores(q_blk, k_blk, first_pos, blk_start):
    qk_scale = q_blk.shape[-1] ** -0.5
    scores = jnp.einsum("niegd,njed->negij", q_blk, k_blk, preferred_element_type=jnp.float32) * qk_scale
    return jnp.where(band_mask(first_pos, blk_start), scores, -1e30)


def attend_forward(queries, keys_ext, values_ext, sink_loc, first_pos):
    n_rows, q_len, kv_loc, group_size, head_dim = queries.shape
    sink_col = sink_loc.reshape(1, kv_loc, group_size, 1)

    def block_body(block_idx, loop_carry):
        out_acc, norm_acc = loop_carry
        blk_start = block_idx * WINDOW
        q_blk = lax.dynamic_slice_in_dim(queries, blk_start, WINDOW, axis=1)
        k_blk = lax.dynamic_slice_in_dim(keys_ext, blk_start, 2 * WINDOW, axis=1)
        v_blk = lax.dynamic_slice_in_dim(values_ext, blk_start, 2 * WINDOW, axis=1)
        scores = block_scores(q_blk, k_blk, first_pos, blk_start)
        row_max = jnp.maximum(jnp.max(scores, axis=-1), sink_col)
        exp_scores = jnp.exp(scores - row_max[..., None])
        row_denom = jnp.sum(exp_scores, axis=-1) + jnp.exp(sink_col - row_max)
        attn_probs = (exp_scores / row_denom[..., None]).astype(jnp.bfloat16)
        out_blk = jnp.einsum("negij,njed->niegd", attn_probs, v_blk, preferred_element_type=jnp.float32)
        out_acc = lax.dynamic_update_slice_in_dim(out_acc, out_blk.astype(jnp.bfloat16), blk_start, axis=1)
        norm_acc = lax.dynamic_update_slice_in_dim(norm_acc, row_max + jnp.log(row_denom), blk_start, axis=3)
        return out_acc, norm_acc

    init_carry = (jnp.zeros(queries.shape, jnp.bfloat16), jnp.zeros((n_rows, kv_loc, group_size, q_len), jnp.float32))
    return lax.fori_loop(0, q_len // WINDOW, block_body, init_carry)


def attend_backward(queries, keys_ext, values_ext, sink_loc, first_pos, log_norm, d_out):
    n_rows, q_len, kv_loc, group_size, head_dim = queries.shape
    qk_scale = head_dim ** -0.5
    sink_col = sink_loc.reshape(1, kv_loc, group_size, 1)

    def block_body(block_idx, loop_carry):
        dq_acc, dk_acc, dv_acc, dsink_acc = loop_carry
        blk_start = block_idx * WINDOW
        q_blk = lax.dynamic_slice_in_dim(queries, blk_start, WINDOW, axis=1)
        k_blk = lax.dynamic_slice_in_dim(keys_ext, blk_start, 2 * WINDOW, axis=1)
        v_blk = lax.dynamic_slice_in_dim(values_ext, blk_start, 2 * WINDOW, axis=1)
        do_blk = lax.dynamic_slice_in_dim(d_out, blk_start, WINDOW, axis=1)
        norm_blk = lax.dynamic_slice_in_dim(log_norm, blk_start, WINDOW, axis=3)
        attn_probs = jnp.exp(block_scores(q_blk, k_blk, first_pos, blk_start) - norm_blk[..., None])
        dv_blk = jnp.einsum("negij,niegd->njed", attn_probs.astype(jnp.bfloat16), do_blk, preferred_element_type=jnp.float32)
        d_probs = jnp.einsum("niegd,njed->negij", do_blk, v_blk, preferred_element_type=jnp.float32).astype(jnp.bfloat16).astype(jnp.float32)
        row_dot = jnp.sum(attn_probs * d_probs, axis=-1)
        d_scores = (attn_probs * (d_probs - row_dot[..., None])).astype(jnp.bfloat16)
        sink_probs = jnp.exp(sink_col - norm_blk)
        dsink_acc = dsink_acc - jnp.sum(sink_probs * row_dot, axis=(0, 3))
        dq_blk = jnp.einsum("negij,njed->niegd", d_scores, k_blk, preferred_element_type=jnp.float32) * qk_scale
        dk_blk = jnp.einsum("negij,niegd->njed", d_scores, q_blk, preferred_element_type=jnp.float32) * qk_scale
        dq_acc = lax.dynamic_update_slice_in_dim(dq_acc, dq_blk.astype(jnp.bfloat16), blk_start, axis=1)
        dk_acc = lax.dynamic_update_slice_in_dim(dk_acc, lax.dynamic_slice_in_dim(dk_acc, blk_start, 2 * WINDOW, axis=1) + dk_blk, blk_start, axis=1)
        dv_acc = lax.dynamic_update_slice_in_dim(dv_acc, lax.dynamic_slice_in_dim(dv_acc, blk_start, 2 * WINDOW, axis=1) + dv_blk, blk_start, axis=1)
        return dq_acc, dk_acc, dv_acc, dsink_acc

    init_carry = (jnp.zeros(queries.shape, jnp.bfloat16), jnp.zeros(keys_ext.shape, jnp.float32), jnp.zeros(values_ext.shape, jnp.float32), jnp.zeros((kv_loc, group_size), jnp.float32))
    dq_all, dk_all, dv_all, dsink_all = lax.fori_loop(0, q_len // WINDOW, block_body, init_carry)
    return dq_all, dk_all, dv_all, dsink_all.reshape(-1)


def norm_backward(d_normed, resid_f32, inv_rms, norm_gain, grad_loc):
    d_normed = d_normed.astype(jnp.bfloat16).astype(jnp.float32)
    gain_grad = d_normed * norm_gain
    d_resid = inv_rms * (gain_grad - resid_f32 * inv_rms * inv_rms * jnp.mean(gain_grad * resid_f32, axis=-1, keepdims=True))
    grad_resid = (grad_loc.astype(jnp.float32) + d_resid).astype(jnp.bfloat16)
    grad_gain = jnp.sum(d_normed * resid_f32 * inv_rms, axis=(0, 1))
    return grad_resid, grad_gain


def solution(mesh):
    act_spec = P("fsdp", "tp", None)
    wout_spec = P(("tp", "fsdp"), None)
    in_specs = (act_spec, act_spec, P(), P("fsdp", "tp"), P("tp"), P("tp"), wout_spec, P())
    out_specs = (act_spec, act_spec, P(), P("fsdp", "tp"), P("tp"), P("tp"), wout_spec, P())

    def device_step(resid_loc, grad_loc, norm_gain, wqkv_loc, bqkv_loc, sink_loc, wout_loc, b_out):
        n_rows = resid_loc.shape[0]
        heads_loc = sink_loc.shape[0]
        resid_f32 = resid_loc.astype(jnp.float32)
        inv_rms = lax.rsqrt(jnp.mean(resid_f32 * resid_f32, axis=-1, keepdims=True) + EPS)
        normed = (resid_f32 * inv_rms * norm_gain).astype(jnp.bfloat16)

        wqkv_full = lax.all_gather(wqkv_loc, "fsdp", axis=0, tiled=True)
        wout_full = lax.all_gather(wout_loc, "fsdp", axis=0, tiled=True)
        normed_all = lax.all_gather(normed, "tp", axis=1, tiled=True)
        seq_len = normed_all.shape[1]
        head_dim = wout_full.shape[0] // heads_loc
        kv_loc = (wqkv_full.shape[1] // head_dim - heads_loc) // 2

        qkv_proj = (jnp.dot(normed_all, wqkv_full, preferred_element_type=jnp.float32) + bqkv_loc.astype(jnp.float32)).astype(jnp.bfloat16)
        positions = jnp.arange(seq_len)
        queries, keys_rot, values = split_qkv(qkv_proj, positions, kv_loc, head_dim)
        pad_zeros = jnp.zeros((n_rows, WINDOW, kv_loc, head_dim), jnp.bfloat16)
        keys_ext = jnp.concatenate([pad_zeros, keys_rot], axis=1)
        values_ext = jnp.concatenate([pad_zeros, values], axis=1)
        attn_out, log_norm = attend_forward(queries, keys_ext, values_ext, sink_loc, 0)
        attn_flat = attn_out.reshape(n_rows, seq_len, heads_loc * head_dim)
        part_sum = jnp.dot(attn_flat, wout_full, preferred_element_type=jnp.float32)
        proj_out = lax.psum_scatter(part_sum, "tp", scatter_dimension=1, tiled=True)
        resid_out = (resid_f32 + proj_out + b_out.astype(jnp.float32)).astype(jnp.bfloat16)

        grad_bout = lax.psum(jnp.sum(grad_loc, axis=(0, 1), dtype=jnp.float32), ("fsdp", "tp"))
        grad_all = lax.all_gather(grad_loc, "tp", axis=1, tiled=True)
        wout_part = jnp.einsum("nth,ntk->hk", attn_flat, grad_all, preferred_element_type=jnp.float32)
        grad_wout = lax.psum_scatter(wout_part, "fsdp", scatter_dimension=0, tiled=True)
        d_attn = jnp.einsum("ntk,hk->nth", grad_all, wout_full, preferred_element_type=jnp.float32).astype(jnp.bfloat16)
        dq_rot, dk_ext, dv_ext, sink_part = attend_backward(queries, keys_ext, values_ext, sink_loc, 0, log_norm, d_attn.reshape(attn_out.shape))
        cos_tab, sin_tab = rope_tables(positions, head_dim)
        d_query = rope_back(dq_rot.astype(jnp.float32), cos_tab[:, None, None], sin_tab[:, None, None]).astype(jnp.bfloat16)
        d_key = rope_back(dk_ext[:, WINDOW:].astype(jnp.bfloat16).astype(jnp.float32), cos_tab[:, None], sin_tab[:, None]).astype(jnp.bfloat16)
        d_value = dv_ext[:, WINDOW:].astype(jnp.bfloat16)
        d_qkv = jnp.concatenate([d_query, d_key[:, :, :, None], d_value[:, :, :, None]], axis=3).reshape(qkv_proj.shape)
        wqkv_part = jnp.einsum("ntd,ntc->dc", normed_all, d_qkv, preferred_element_type=jnp.float32)
        grad_wqkv = lax.psum_scatter(wqkv_part, "fsdp", scatter_dimension=0, tiled=True)
        grad_bqkv = lax.psum(jnp.sum(d_qkv, axis=(0, 1), dtype=jnp.float32), "fsdp")
        grad_sinks = lax.psum(sink_part, "fsdp")
        normed_part = jnp.einsum("ntc,dc->ntd", d_qkv, wqkv_full, preferred_element_type=jnp.float32)
        d_normed = lax.psum_scatter(normed_part, "tp", scatter_dimension=1, tiled=True)
        grad_resid, gain_part = norm_backward(d_normed, resid_f32, inv_rms, norm_gain, grad_loc)
        grad_gain = lax.psum(gain_part, ("fsdp", "tp"))
        return (resid_out, grad_resid, grad_gain, grad_wqkv, grad_bqkv, grad_sinks, grad_wout, grad_bout)

    return jax.shard_map(device_step, mesh=mesh, in_specs=in_specs, out_specs=out_specs, check_vma=False)
```

profile of v0, /device:TPU:0, one launch (start us, length us, event | category | flops | bytes accessed | tf_op | source)
XLA Modules:
  0.0 962.0 jit_solution(16917804507916723677)
XLA Ops:
  13.6 66.8 %all-gather.12.cloned.1.call-done = bf16[64,12,1536]{2,1,0:T(8,128)(2,1)} async-done(((bf16[1,12,1536]{2,1,0:T(8,128)(2,1)}), bf16[64,12,1536]{2,1,0:T(8,128)(2,1)}) %all-gather.12.cloned.1.call-update) | async-done | bytes 2359312 | tf_op jit(solution)/shard_map/all_gather | solution.py:132
  80.4 4.9 reshape.900
  85.3 11.7 %all-gather.10.cloned.1.call-done = bf16[1,1536,1536]{2,1,0:T(8,128)(2,1)} async-done(((bf16[1,768,1536]{2,1,0:T(8,128)(2,1)}), bf16[1,1536,1536]{2,1,0:T(8,128)(2,1)}) %all-gather.10.cloned.1.call-update) | async-done | bytes 4718608 | tf_op jit(solution)/shard_map/all_gather | solution.py:151
  97.0 8.3 fusion.86
  105.3 12.8 %all-gather.6.cloned.1.call-done = bf16[1,1536,1536]{2,1,0:T(8,128)(2,1)} async-done(((bf16[1,768,1536]{2,1,0:T(8,128)(2,1)}), bf16[1,1536,1536]{2,1,0:T(8,128)(2,1)}) %all-gather.6.cloned.1.call-update) | async-done | bytes 4718608 | tf_op jit(solution)/shard_map/all_gather | solution.py:133
  118.1 71.1 %all-gather.8.cloned.1.call-done = bf16[1536,1024]{1,0:T(8,128)(2,1)} async-done(((bf16[24,1024]{1,0:T(8,128)(2,1)}), bf16[1536,1024]{1,0:T(8,128)(2,1)}) %all-gather.8.cloned.1.call-update) | async-done | bytes 3145744 | tf_op jit(solution)/shard_map/all_gather | solution.py:131
  189.3 8.2 add_convert_fusion
  201.5 4.4 copy.50
  211.7 42.4 %while.39 = (s32[]{:T(128)}, bf16[1,1536,1,6,128]{1,4,3,2,0:T(8,128)(2,1)}, f32[1,1,6,1536]{3,2,1,0:T(8,128)S(1)}, bf16[1,1664,1,128]{1,3,2,0:T(8,128)(2,1)}, bf...) while((s32[]{:T(128)}, ...), condition=%wide.region_4.5_spmd, body=%wide.region_1.4_spmd.sunk | while | flops 102470792 | bytes 2994456 | solution.py:74
  257.7 105.0 %while.40 = (s32[]{:T(128)}, bf16[1,1536,1,6,128]{1,4,3,2,0:T(8,128)(2,1)}, f32[1,1664,1,128]{1,3,2,0:T(8,128)}, f32[1,1664,1,128]{1,3,2,0:T(8,128)}, f32[1,6]{1...) while((s32[]{:T(128)}, ...), condition=%wide.region_9.10_spmd.clone, body=%wide.region_6.9_spmd.clone.sunk | while | flops 254249104 | bytes 7691174 | solution.py:105
  374.1 7.8 convolution_bitcast_fusion.2
  382.0 9.9 %convolution_bitcast_fusion.3 = f32[1,1536,1536]{2,1,0:T(8,128)} fusion(bf16[1536,768]{0,1:T(8,128)(2,1)} %bitcast.264, bf16[768,1536]{1,0:T(8,128)(2,1)} %reshape.900), kind=kOutput, calls=%fused_computation.94 | convolution fusion | flops 3623878656 | bytes 14155776 | tf_op jit(solution)/shard_map/dot_general | solution.py:146
  391.9 9.9 %fusion.80 = f32[1536,1024]{1,0:T(8,128)} fusion(bf16[1536,1024]{0,1:T(8,128)(2,1)} %bitcast.263, bf16[1,1536,1536]{2,1,0:T(8,128)(2,1)} %all-gather.6.cloned.1.call-done), kind=kOutput, calls=%fused_computation.117 | convolution fusion | flops 4831838208 | bytes 14155776 | tf_op jit(solution)/shard_map/ntd,ntc->dc/dot_general | solution.py:161
  401.9 9.0 fusion.76
  410.8 209.7 %fusion = f32[16,1536]{1,0:T(8,128)} fusion(f32[768,1536]{1,0:T(8,128)} %fusion.76), kind=kCustom, calls=%all-reduce-scatter | all-reduce-scatter fusion | flops 1572865 | bytes 4817408
  625.9 4.4 collective-permute-start
  638.6 5.1 collective-permute-start.14
  643.8 9.2 collective-permute-start.2
  663.4 4.3 collective-permute-start.6
  673.0 4.3 collective-permute-start.9
  677.9 175.3 %all-reduce.5 = (f32[1024]{0:T(1024)}, f32[6]{0:T(128)}) all-reduce(f32[1024]{0:T(1024)S(1)} %bitcast.278, f32[6]{0:T(128)S(1)} %bitcast.277), channel_id=1, replica_groups=mesh['tp'=2,'fsdp'=64] {'fsdp'}, use_global_device_ids=true, to_apply=%region_16.17 | all-reduce | flops 1030 | bytes 8240 | tf_op jit(solution)/shard_map/psum | solution.py:163
  853.2 26.6 %concatenate.120 = f32[268,1536]{1,0:T(8,128)} concatenate(f32[12,1536]{1,0:T(8,128)} %collective-permute-done.15, f32[16,1536]{1,0:T(8,128)S(1)} %collective-permute-done.14, f32[16,1536]{1,0:T(8,128)S(1)} %collective-permute-done.13, f32[16,1536]{1,0:T(8,128)} %copy-done.19, f32[16,1536]{1,0:T(8,128)} %copy-done.18, f32[16,1536]{1,0:T(8,128)} %copy-done.17, ...), dimensions={0} | concatenate | bytes 3293184
  885.3 7.1 convert_reduce_fusion.1
  892.4 62.8 %all-reduce.4 = (f32[1536]{0:T(1024)}, f32[1536]{0:T(1024)}) all-reduce(f32[1536]{0:T(1024)S(1)} %get-tuple-element.548, f32[1536]{0:T(1024)S(1)} %get-tuple-element.600), channel_id=1, replica_groups=mesh['tp'=2,'fsdp'=64] {'fsdp','tp'}, use_global_device_ids=true, to_apply=%region_13.14 | all-reduce | flops 3072 | bytes 24576 | tf_op jit(solution)/shard_map/psum | solution.py:168
  (393 shorter events, 211.4 us)
Async XLA Ops:
  7.2 73.2 %all-gather.12.cloned.1.call-start = ((), (), s32[]{:S(2)}) async-start(), calls=%async_computation.9 | async-start | bytes 3194880 | tf_op jit(solution)/shard_map/all_gather | solution.py:132
  7.9 89.1 %all-gather.10.cloned.1.call-start = ((), (), s32[]{:S(2)}) async-start(), calls=%async_computation.6 | async-start | bytes 7077888 | tf_op jit(solution)/shard_map/all_gather | solution.py:151
  8.7 109.5 %all-gather.6.cloned.1.call-start = ((), (), s32[]{:S(2)}) async-start(), calls=%async_computation.3 | async-start | bytes 7077888 | tf_op jit(solution)/shard_map/all_gather | solution.py:133
  11.4 177.8 %all-gather.8.cloned.1.call-start = ((), (), s32[]{:S(2)}) async-start(), calls=%async_computation.4 | async-start | bytes 3194880 | tf_op jit(solution)/shard_map/all_gather | solution.py:131
  12.0 869.4 %reduce-scatter.8.cloned.1.call-start = ((), (), s32[]{:S(2)}) async-start(), calls=%async_computation.7 | async-start | bytes 14155776 | tf_op jit(solution)/shard_map/reduce_scatter | solution.py:166
  381.9 503.3 %reduce-scatter.6.cloned.1.call-start = ((), (), s32[]{:S(2)}) async-start(), calls=%async_computation.5 | async-start | bytes 14155776 | tf_op jit(solution)/shard_map/reduce_scatter | solution.py:147
  391.9 563.3 %reduce-scatter.10.cloned.1.call-start = ((), (), s32[]{:S(2)}) async-start(), calls=%async_computation.8 | async-start | bytes 6389760 | tf_op jit(solution)/shard_map/reduce_scatter | solution.py:162
  622.0 12.5 %collective-permute-start.15 = (f32[12,1536]{1,0:T(8,128)}, f32[12,1536]{1,0:T(8,128)}, u32[]{:S(2)}, u32[]{:S(2)}) collective-permute-start(f32[12,1536]{1,0:T(8,128)} %slice.67), channel_id=1, source_target_pairs={{0,16},{1,17},{2,18},{3,19},{4,20},{5,21},{6,22},{7,23},{8,24},{9,... | collective-permute-start | bytes 221192
  625.9 11.4 %collective-permute-start = (f32[16,1536]{1,0:T(8,128)}, f32[16,1536]{1,0:T(8,128)S(1)}, u32[]{:S(2)}, u32[]{:S(2)}) collective-permute-start(f32[16,1536]{1,0:T(8,128)} %fusion), channel_id=1, source_target_pairs={{0,1},{1,2},{2,3},{3,4},{4,5},{5,6},{6,7},{7,8},{8,9},{9,10},{10,1... | collective-permute-start | bytes 294920
  630.3 8.3 collective-permute-start.1
  631.9 11.9 %collective-permute-start.10 = (f32[16,1536]{1,0:T(8,128)}, f32[16,1536]{1,0:T(8,128)S(1)}, u32[]{:S(2)}, u32[]{:S(2)}) collective-permute-start(f32[16,1536]{1,0:T(8,128)} %fusion), channel_id=1, source_target_pairs={{0,11},{1,12},{2,13},{3,14},{4,15},{5,16},{6,17},{7,18},{8,19},{9,... | collective-permute-start | bytes 294920
  633.2 19.9 %collective-permute-start.11 = (f32[16,1536]{1,0:T(8,128)}, f32[16,1536]{1,0:T(8,128)S(1)}, u32[]{:S(2)}, u32[]{:S(2)}) collective-permute-start(f32[16,1536]{1,0:T(8,128)} %fusion), channel_id=1, source_target_pairs={{0,12},{1,13},{2,14},{3,15},{4,16},{5,17},{6,18},{7,19},{8,20},{9,... | collective-permute-start | bytes 294920
  634.5 21.6 %collective-permute-start.12 = (f32[16,1536]{1,0:T(8,128)}, f32[16,1536]{1,0:T(8,128)S(1)}, u32[]{:S(2)}, u32[]{:S(2)}) collective-permute-start(f32[16,1536]{1,0:T(8,128)} %fusion), channel_id=1, source_target_pairs={{0,13},{1,14},{2,15},{3,16},{4,17},{5,18},{6,19},{7,20},{8,21},{9,... | collective-permute-start | bytes 294920
  637.3 22.4 %collective-permute-start.13 = (f32[16,1536]{1,0:T(8,128)}, f32[16,1536]{1,0:T(8,128)S(1)}, u32[]{:S(2)}, u32[]{:S(2)}) collective-permute-start(f32[16,1536]{1,0:T(8,128)} %fusion), channel_id=1, source_target_pairs={{0,14},{1,15},{2,16},{3,17},{4,18},{5,19},{6,20},{7,21},{8,22},{9,... | collective-permute-start | bytes 294920
  638.6 24.7 %collective-permute-start.14 = (f32[16,1536]{1,0:T(8,128)}, f32[16,1536]{1,0:T(8,128)S(1)}, u32[]{:S(2)}, u32[]{:S(2)}) collective-permute-start(f32[16,1536]{1,0:T(8,128)} %fusion), channel_id=1, source_target_pairs={{0,15},{1,16},{2,17},{3,18},{4,19},{5,20},{6,21},{7,22},{8,23},{9,... | collective-permute-start | bytes 294920
  643.8 23.9 %collective-permute-start.2 = (f32[16,1536]{1,0:T(8,128)}, f32[16,1536]{1,0:T(8,128)S(1)}, u32[]{:S(2)}, u32[]{:S(2)}) collective-permute-start(f32[16,1536]{1,0:T(8,128)} %fusion), channel_id=1, source_target_pairs={{0,3},{1,4},{2,5},{3,6},{4,7},{5,8},{6,9},{7,10},{8,11},{9,12},{10... | collective-permute-start | bytes 294920
  653.1 17.8 %collective-permute-start.3 = (f32[16,1536]{1,0:T(8,128)}, f32[16,1536]{1,0:T(8,128)S(1)}, u32[]{:S(2)}, u32[]{:S(2)}) collective-permute-start(f32[16,1536]{1,0:T(8,128)} %fusion), channel_id=1, source_target_pairs={{0,4},{1,5},{2,6},{3,7},{4,8},{5,9},{6,10},{7,11},{8,12},{9,13},{1... | collective-permute-start | bytes 294920
  656.2 16.9 %collective-permute-start.4 = (f32[16,1536]{1,0:T(8,128)}, f32[16,1536]{1,0:T(8,128)S(1)}, u32[]{:S(2)}, u32[]{:S(2)}) collective-permute-start(f32[16,1536]{1,0:T(8,128)} %fusion), channel_id=1, source_target_pairs={{0,5},{1,6},{2,7},{3,8},{4,9},{5,10},{6,11},{7,12},{8,13},{9,14},{... | collective-permute-start | bytes 294920
  659.6 221.8 %copy-start.21 = (f32[1536]{0:T(1024)S(1)}, f32[1536]{0:T(1024)}, u32[]{:S(2)}) copy-start(f32[1536]{0:T(1024)} %param.14) | copy-start | bytes 18436
  659.7 193.5 %collective-permute-start.5 = (f32[16,1536]{1,0:T(8,128)}, f32[16,1536]{1,0:T(8,128)S(1)}, u32[]{:S(2)}, u32[]{:S(2)}) collective-permute-start(f32[16,1536]{1,0:T(8,128)} %fusion), channel_id=1, source_target_pairs={{0,6},{1,7},{2,8},{3,9},{4,10},{5,11},{6,12},{7,13},{8,14},{9,15},... | collective-permute-start | bytes 294920
  663.4 189.8 %collective-permute-start.6 = (f32[16,1536]{1,0:T(8,128)}, f32[16,1536]{1,0:T(8,128)S(1)}, u32[]{:S(2)}, u32[]{:S(2)}) collective-permute-start(f32[16,1536]{1,0:T(8,128)} %fusion), channel_id=1, source_target_pairs={{0,7},{1,8},{2,9},{3,10},{4,11},{5,12},{6,13},{7,14},{8,15},{9,16}... | collective-permute-start | bytes 294920
  667.7 185.5 %collective-permute-start.7 = (f32[16,1536]{1,0:T(8,128)}, f32[16,1536]{1,0:T(8,128)S(1)}, u32[]{:S(2)}, u32[]{:S(2)}) collective-permute-start(f32[16,1536]{1,0:T(8,128)} %fusion), channel_id=1, source_target_pairs={{0,8},{1,9},{2,10},{3,11},{4,12},{5,13},{6,14},{7,15},{8,16},{9,17... | collective-permute-start | bytes 294920
  670.8 182.4 %collective-permute-start.8 = (f32[16,1536]{1,0:T(8,128)}, f32[16,1536]{1,0:T(8,128)S(1)}, u32[]{:S(2)}, u32[]{:S(2)}) collective-permute-start(f32[16,1536]{1,0:T(8,128)} %fusion), channel_id=1, source_target_pairs={{0,9},{1,10},{2,11},{3,12},{4,13},{5,14},{6,15},{7,16},{8,17},{9,1... | collective-permute-start | bytes 294920
  673.0 180.2 %collective-permute-start.9 = (f32[16,1536]{1,0:T(8,128)}, f32[16,1536]{1,0:T(8,128)S(1)}, u32[]{:S(2)}, u32[]{:S(2)}) collective-permute-start(f32[16,1536]{1,0:T(8,128)} %fusion), channel_id=1, source_target_pairs={{0,10},{1,11},{2,12},{3,13},{4,14},{5,15},{6,16},{7,17},{8,18},{9,... | collective-permute-start | bytes 294920
  (29 other events, 1019.2 us)
Sparse Core Ops, SparseCore 0:
  10.7 69.6 all-gather.11
  82.1 14.8 all-gather.9
  99.2 18.8 all-gather.5
  120.8 68.4 all-gather.7
  382.0 16.5 reduce-scatter.7
  400.9 20.6 reduce-scatter.5
  426.6 248.7 reduce-scatter.9
where the time goes:
time: 967 us; the launch traced here: 962 us
  blocking collectives  448 us (46%)
  matrix products  189 us (20%)
  waiting for transfers between devices  164 us (17%)
  local copies, waits for them, and re-layouts  51.9 us (5%)
  starting transfers between devices  51.8 us (5%)
  other arithmetic  40.4 us (4%)
  between operations  15.5 us (2%)
    unnamed x1, blocking collectives  210 us
    psum x1, blocking collectives, device_step(): grad_bqkv = lax.psum(jnp.sum(d_qkv, axis=(0, 1), dtype=jnp.float32), 'fsdp')  175 us
    all_gather x1, waiting for transfers between devices, device_step(): wqkv_full = lax.all_gather(wqkv_loc, 'fsdp', axis=0, tiled=True)  71.1 us
    all_gather x1, waiting for transfers between devices, device_step(): wout_full = lax.all_gather(wout_loc, 'fsdp', axis=0, tiled=True)  66.8 us
    psum x1, blocking collectives, device_step(): grad_gain = lax.psum(gain_part, ('fsdp', 'tp'))  62.8 us
    unnamed x16, starting transfers between devices  51.5 us
    unnamed x66, local copies, waits for them, and re-layouts  39.3 us
    dot_general x24, matrix products, block_scores(): jnp.einsum('niegd,njed->negij', q_blk, k_blk, preferred_element_type=jnp....  31.1 us
  transfers between devices with their start and end apart: 23, of which 4 were waited for; matrix products, arithmetic and copies ran while one was open for 31% of the time, Pallas kernels for 0%

commit v1 on v0

v1 whole, which is shorter than its diff:
```python
import jax
import jax.numpy as jnp
from jax import lax
from jax.experimental import pallas as pl
from jax.experimental.pallas import tpu as pltpu
from jax.sharding import PartitionSpec as P

EPS = 1e-5
ROPE_BASE = 150000.0
WINDOW = 128
MESH = pl.DeviceIdType.MESH
STRIDE = (16, 4, 1)
F32 = jnp.float32
BF16 = jnp.bfloat16
VMEM_LIMIT = 67_000_000
Z, Y, X = range(3)
UP, DOWN, FAR = 1, -1, 2
L = 128
NEG = -1e30


def coord(dim):
    return lax.rem(lax.div(lax.axis_index("fsdp"), STRIDE[dim]), 4)


def shifted(dim, k):
    return lax.rem(coord(dim) + (k + 4), 4)


def peer(dim, k):
    f = lax.axis_index("fsdp")
    return {"fsdp": f + (shifted(dim, k) - coord(dim)) * STRIDE[dim]}


def partner():
    return {"tp": 1 - lax.axis_index("tp")}


def entry_barrier(peers):
    barrier = pltpu.get_barrier_semaphore()
    for p in peers:
        pl.semaphore_signal(barrier, inc=1, device_id=p, device_id_type=MESH)
    pl.semaphore_wait(barrier, len(peers))


def ring_peers():
    return [peer(dim, k) for dim in range(3) for k in (UP, DOWN)]


class Copies:
    def __init__(self, send_sem, recv_sem):
        self.send_sem, self.recv_sem = send_sem, recv_sem
        self.n = 0
        self.sent = []

    def slots(self, count):
        first = self.n
        self.n += count
        return first

    def make(self, src, dst, slot, device):
        return pltpu.make_async_remote_copy(src_ref=src, dst_ref=dst, send_sem=self.send_sem.at[slot], recv_sem=self.recv_sem.at[slot], device_id=device, device_id_type=MESH)

    def send(self, src, dst, slot, device):
        copy = self.make(src, dst, slot, device)
        copy.start()
        self.sent.append(copy)

    def arrive(self, ref, slot, device):
        self.make(ref, ref, slot, device).wait_recv()

    def drain(self):
        for copy in self.sent:
            copy.wait_send()
        self.sent = []


class GatherStage:
    def __init__(self, copies, dim, slot_view, own_view):
        self.c, self.dim, self.view, self.own = copies, dim, slot_view, own_view
        self.base = copies.slots(6)

    def start(self):
        me = coord(self.dim)
        for h in (0, 1):
            self.c.send(self.own(h), self.view(me, h), self.base + h, peer(self.dim, UP))
            self.c.send(self.own(1 - h), self.view(me, 1 - h), self.base + 3 - h, peer(self.dim, DOWN))

    def sides(self):
        return [(shifted(self.dim, k), peer(self.dim, k)) for k in (DOWN, UP)]

    def mid(self):
        (lo, down), (hi, up) = self.sides()
        self.c.arrive(self.view(lo, 0), self.base, down)
        self.c.send(self.view(lo, 0), self.view(lo, 0), self.base + 4, up)
        self.c.arrive(self.view(hi, 1), self.base + 3, up)
        self.c.send(self.view(hi, 1), self.view(hi, 1), self.base + 5, down)

    def finish(self):
        (lo, down), (hi, up) = self.sides()
        far = shifted(self.dim, FAR)
        for n, (at, h, dev) in enumerate(((lo, 1, down), (hi, 0, up))):
            self.c.arrive(self.view(at, h), self.base + 1 + n, dev)
            self.c.arrive(self.view(far, n), self.base + 4 + n, dev)


def gather_stages(copies, in_ref, out_ref, order, cols):
    half_cols = [pl.ds(cols[0], cols[1]), pl.ds(cols[0] + cols[1], cols[2])]
    stages = []
    for n in range(3):
        def view(c, h, n=n):
            idx = []
            for dim in range(3):
                if dim == order[n]:
                    idx.append(c)
                elif dim in order[:n]:
                    idx.append(slice(None))
                else:
                    idx.append(coord(dim))
            return out_ref.at[tuple(idx) + (slice(None), half_cols[h])]
        if n == 0:
            own = lambda h: in_ref.at[:, half_cols[h]]
        else:
            own = lambda h, n=n, view=view: view(coord(order[n]), h)
        stages.append(GatherStage(copies, order[n], view, own))
    return stages


def gather_kernel(wq_in, wo_in, x_ref, dy_ref, g_ref, wq_out, wo_out, h_all, dy_all, wq_oth, wo_oth, h_own, send_sem, recv_sem, loc_sem):
    tp = lax.axis_index("tp")
    for ref, own in ((wq_out, wq_in), (wo_out, wo_in)):
        ref[coord(Z), coord(Y), coord(X)] = own[...]
    entry_barrier(ring_peers() + [partner()])
    copies = Copies(send_sem, recv_sem)
    jobs = [gather_stages(copies, wq_in, wq_out, (X, Y, Z), (0, 256, L)), gather_stages(copies, wq_in, wq_out, (Y, Z, X), (384, L, 256)),
            gather_stages(copies, wq_in, wq_out, (Z, X, Y), (768, L, L))]
    jobs += [gather_stages(copies, wo_in, wo_out, order, (n * 256, L, L)) for n, order in enumerate(((X, Y, Z), (Y, Z, X), (Z, X, Y)))]
    for job in jobs:
        job[0].start()
    local = [pltpu.make_async_copy(dy_ref, dy_all.at[tp], loc_sem.at[0])]
    local[0].start()
    slot_dy = copies.slots(1)
    copies.send(dy_ref, dy_all.at[tp], slot_dy, partner())
    rows = x_ref.shape[0]
    parts = 6
    slot_h = copies.slots(parts)
    step = rows // parts
    gain = g_ref[...]

    def norm_part(k):
        @pl.loop(0, step // 32)
        def _(i):
            at = pl.ds(k * step + i * 32, 32)
            xv = x_ref[at, :].astype(F32)
            inv = lax.rsqrt(jnp.mean(xv * xv, axis=-1, keepdims=True) + EPS)
            h_own[at, :] = (xv * inv * gain).astype(BF16)

    def send_part(k):
        at = pl.ds(k * step, step)
        copy = pltpu.make_async_copy(h_own.at[at, :], h_all.at[tp, at, :], loc_sem.at[1 + k])
        copy.start()
        local.append(copy)
        copies.send(h_own.at[at, :], h_all.at[tp, at, :], slot_h + k, partner())

    part = 0
    for n in range(3):
        for phase in range(2):
            norm_part(part)
            if part > 0:
                send_part(part - 1)
            part += 1
            for job in jobs:
                if phase == 0:
                    job[n].mid()
                else:
                    job[n].finish()
                    if n < 2:
                        job[n + 1].start()
    send_part(parts - 1)
    slot_w = copies.slots(2)
    copies.send(wq_out, wq_oth, slot_w, partner())
    copies.send(wo_out, wo_oth, slot_w + 1, partner())
    oth = 1 - tp
    copies.arrive(dy_all.at[oth], slot_dy, partner())
    for k in range(parts):
        copies.arrive(h_all.at[oth, pl.ds(k * step, step), :], slot_h + k, partner())
    copies.arrive(wq_oth, slot_w, partner())
    copies.arrive(wo_oth, slot_w + 1, partner())
    copies.drain()
    for copy in local:
        copy.wait()


VM = pl.BlockSpec(memory_space=pltpu.VMEM)
ANY = pl.BlockSpec(memory_space=pl.ANY)


def gather_all(wq_in, wo_in, x, dy, gain):
    rows, d = x.shape
    wq_shape = jax.ShapeDtypeStruct((4, 4, 4) + wq_in.shape, BF16)
    wo_shape = jax.ShapeDtypeStruct((4, 4, 4) + wo_in.shape, BF16)
    act = jax.ShapeDtypeStruct((2, rows, d), BF16)
    n = 6 * 18 + 1 + 6 + 2
    return pl.pallas_call(
        gather_kernel, name="gather_all",
        out_shape=(wq_shape, wo_shape, act, act, wq_shape, wo_shape),
        in_specs=[VM] * 5, out_specs=(VM, VM, ANY, ANY, ANY, ANY),
        scratch_shapes=[pltpu.VMEM((rows, d), BF16), pltpu.SemaphoreType.DMA((n,)), pltpu.SemaphoreType.DMA((n,)), pltpu.SemaphoreType.DMA((7,))],
        compiler_params=pltpu.CompilerParams(collective_id=0, has_side_effects=True, vmem_limit_bytes=VMEM_LIMIT),
    )(wq_in, wo_in, x, dy, gain)


def rotate(vals, cos, sin):
    return vals * cos + pltpu.roll(vals, 64, 1) * sin


def stack_heads(ref, heads):
    return jnp.concatenate([ref[:, i * L:(i + 1) * L] for i in range(heads)], axis=0)


def dot_tn(a, b):
    return lax.dot_general(a, b, (((0,), (0,)), ((), ())), preferred_element_type=F32)


def dot_nt(a, b):
    return lax.dot_general(a, b, (((1,), (1,)), ((), ())), preferred_element_type=F32)


def attend_kernel(heads, n_blocks, qkv_ref, do_ref, cos_ref, sin_ref, sink_ref, o_ref, dqkv_ref, dsink_ref, k_buf, v_buf, dk_buf, dv_buf, tab_buf):
    i = pl.program_id(0)
    scale = 128.0 ** -0.5
    width = heads * L

    @pl.when(i == 0)
    def _():
        k_buf[...] = jnp.zeros_like(k_buf)
        v_buf[...] = jnp.zeros_like(v_buf)
        dk_buf[...] = jnp.zeros_like(dk_buf)
        dv_buf[...] = jnp.zeros_like(dv_buf)
        dsink_ref[...] = jnp.zeros_like(dsink_ref)

    @pl.when(i > 0)
    def _():
        k_buf[0:L, :] = k_buf[L:2 * L, :]
        v_buf[0:L, :] = v_buf[L:2 * L, :]
        dk_buf[0:L, :] = dk_buf[L:2 * L, :]
        dv_buf[0:L, :] = dv_buf[L:2 * L, :]
        tab_buf[0:2] = tab_buf[2:4]

    cos, sin = cos_ref[...], sin_ref[...]
    tab_buf[2], tab_buf[3] = cos, sin
    cos_all = jnp.concatenate([cos] * heads, axis=0)
    sin_all = jnp.concatenate([sin] * heads, axis=0)
    k_buf[L:2 * L, :] = rotate(qkv_ref[:, width:width + L].astype(F32), cos, sin).astype(BF16)
    v_buf[L:2 * L, :] = qkv_ref[:, width + L:width + 2 * L]
    q = rotate(stack_heads(qkv_ref, heads).astype(F32), cos_all, sin_all).astype(BF16)
    do = stack_heads(do_ref, heads)
    keys, vals = k_buf[...], v_buf[...]
    sink = sink_ref[...]

    scores = dot_nt(keys, q) * scale
    k_idx = lax.broadcasted_iota(jnp.int32, (256, 128), 0)
    q_idx = lax.broadcasted_iota(jnp.int32, (256, 128), 1)
    allowed = (k_idx > q_idx) & (k_idx <= q_idx + WINDOW) & ((k_idx >= WINDOW) | (i > 0))
    bias = jnp.where(allowed, 0.0, NEG)
    scores = scores + jnp.concatenate([bias] * heads, axis=1)
    top = jnp.maximum(jnp.max(scores, axis=0, keepdims=True), sink)
    probs = jnp.exp(scores - top)
    sink_exp = jnp.exp(sink - top)
    inv = 1.0 / (jnp.sum(probs, axis=0, keepdims=True) + sink_exp)
    probs = probs * inv
    probs_b = probs.astype(BF16)
    out = dot_tn(probs_b, vals).astype(BF16)
    for h in range(heads):
        o_ref[:, h * L:(h + 1) * L] = out[h * L:(h + 1) * L, :]
    d_probs = dot_nt(vals, do).astype(BF16).astype(F32)
    row_dot = jnp.sum(probs * d_probs, axis=0, keepdims=True)
    d_scores = (probs * (d_probs - row_dot)).astype(BF16)
    dsink_ref[...] += -(sink_exp * inv * row_dot)
    dv_new = jnp.dot(probs_b, do, preferred_element_type=F32)
    dk_new = jnp.dot(d_scores, q, preferred_element_type=F32) * scale
    dq = (dot_tn(d_scores, keys) * scale).astype(BF16).astype(F32)
    dq = rotate(dq, cos_all, -sin_all).astype(BF16)
    here = pl.ds(pl.multiple_of(i * L, 128), 128)
    for h in range(heads):
        dqkv_ref[here, h * L:(h + 1) * L] = dq[h * L:(h + 1) * L, :]

    dk_prev = dk_buf[0:L, :] + dk_new[0:L, :]
    dv_prev = dv_buf[0:L, :] + dv_new[0:L, :]

    def put(at, dk, dv, c, s):
        dqkv_ref[at, width:width + L] = rotate(dk.astype(BF16).astype(F32), c, -s).astype(BF16)
        dqkv_ref[at, width + L:width + 2 * L] = dv.astype(BF16)

    @pl.when(i > 0)
    def _():
        put(pl.ds(pl.multiple_of((i - 1) * L, 128), 128), dk_prev, dv_prev, tab_buf[0], tab_buf[1])

    dk_buf[L:2 * L, :] = dk_new[L:2 * L, :]
    dv_buf[L:2 * L, :] = dv_new[L:2 * L, :]

    @pl.when(i == n_blocks - 1)
    def _():
        put(here, dk_new[L:2 * L, :], dv_new[L:2 * L, :], cos, sin)


def attend(qkv, d_o, cos, sin, sink_row):
    seq, cols = qkv.shape
    width = d_o.shape[1]
    heads = width // 128
    n_blocks = seq // WINDOW
    def row(c):
        return pl.BlockSpec((WINDOW, c), lambda i: (i, 0))

    def whole(*s):
        return pl.BlockSpec(s, lambda i: (0, 0))

    def kernel(*refs):
        attend_kernel(heads, n_blocks, *refs)

    return pl.pallas_call(
        kernel, name="attend", grid=(n_blocks,),
        out_shape=(jax.ShapeDtypeStruct((seq, width), BF16), jax.ShapeDtypeStruct((seq, cols), BF16), jax.ShapeDtypeStruct((1, width), F32)),
        in_specs=[row(cols), row(width), row(128), row(128), whole(1, width)],
        out_specs=(row(width), whole(seq, cols), whole(1, width)),
        scratch_shapes=[pltpu.VMEM((2 * L, L), t) for t in (BF16, BF16, F32, F32)] + [pltpu.VMEM((4, L, L), F32)],
        compiler_params=pltpu.CompilerParams(dimension_semantics=("arbitrary",), vmem_limit_bytes=VMEM_LIMIT),
    )(qkv, d_o, cos, sin, sink_row)


class ScatterStage:
    def __init__(self, copies, dim, blk, buf, put):
        self.c, self.dim, self.blk, self.buf, self.put = copies, dim, blk, buf, put
        self.base = copies.slots(6)
        self.a_up, self.a_down, self.lo = 0, 1, (2, 3)
        self.hi = (4, 5)

    def send(self, src, slot, k):
        self.c.send(src, self.buf.at[slot], self.base + slot, peer(self.dim, k))

    def arrive(self, slot, k):
        self.c.arrive(self.buf.at[slot], self.base + slot, peer(self.dim, k))

    def start(self):
        up, down, far = (shifted(self.dim, k) for k in (UP, DOWN, FAR))
        self.send(self.blk(far, 0), self.a_up, UP)
        self.send(self.blk(far, 1), self.a_down, DOWN)
        self.send(self.blk(up, 1), self.lo[1], UP)
        self.send(self.blk(down, 0), self.hi[0], DOWN)

    def add(self, slot, src):
        dst = self.buf.at[slot]
        if len(src.shape) == 2:
            dst[...] = dst[...] + src[...]
        else:
            @pl.loop(0, src.shape[0])
            def _(j):
                dst[j] = dst[j] + src[j]

    def mid(self):
        self.arrive(self.a_up, DOWN)
        self.add(self.a_up, self.blk(shifted(self.dim, UP), 0))
        self.arrive(self.a_down, UP)
        self.add(self.a_down, self.blk(shifted(self.dim, DOWN), 1))
        self.send(self.buf.at[self.a_up], self.lo[0], UP)
        self.send(self.buf.at[self.a_down], self.hi[1], DOWN)

    def finish(self):
        me = coord(self.dim)
        for h in (1, 0):
            self.arrive(self.lo[h], DOWN)
            self.arrive(self.hi[1 - h], UP)
        for h in (0, 1):
            own, a, b = self.blk(me, h), self.buf.at[self.lo[h]], self.buf.at[self.hi[h]]
            if len(own.shape) == 2:
                self.put(h, None, own[...] + a[...] + b[...])
            else:
                @pl.loop(0, own.shape[0])
                def _(j):
                    self.put(h, j, own[j] + a[j] + b[j])


class DirectStage:
    def __init__(self, copies, dim, blk, buf, put):
        self.c, self.dim, self.blk, self.buf, self.put = copies, dim, blk, buf, put
        self.base = copies.slots(3)

    def start(self):
        for slot, k in enumerate((UP, DOWN, FAR)):
            self.c.send(self.blk(shifted(self.dim, k)), self.buf.at[slot], self.base + slot, peer(self.dim, k))

    def finish(self):
        for slot, k in enumerate((UP, DOWN, FAR)):
            self.c.arrive(self.buf.at[slot], self.base + slot, peer(self.dim, k))
        b = self.buf
        self.put((self.blk(coord(self.dim))[...] + b[0]) + (b[1] + b[2]))


def scatter_stages(copies, src, out, order, first, width, bufs, padded):
    hw = width // 2
    r1, r2, r3, s2, s3 = bufs
    rows = out.shape[0]
    rest = [dim for dim in range(3) if dim != order[0]]

    def pick(ref, at, t, cols):
        idx = [slice(None)] * (len(ref.shape) - 1)
        idx[at] = t
        return ref.at[tuple(idx) + (cols,)]

    def part(h, base=0):
        return pl.ds(base + h * hw, hw)

    def put1(h, j, val):
        s2[j, ..., part(h)] = val

    def put2(h, j, val):
        if padded:
            for t in range(4):
                s3[t, 0:rows, part(h)] = val[rows * t:rows * t + rows, :]
        else:
            s3[j, :, part(h)] = val

    def put3(val):
        out[:, pl.ds(first, width)] = val[0:rows, :]

    return (ScatterStage(copies, order[0], lambda t, h: pick(src, order[0], t, part(h, first)), r1, put1),
            ScatterStage(copies, order[1], lambda t, h: pick(s2, rest.index(order[1]), t, part(h)), r2, put2),
            DirectStage(copies, order[2], lambda t: s3.at[t], r3, put3))


WO_JOBS = (((Y, Z, X), 0, 768), ((Z, Y, X), 768, 768))
WQ_JOBS = (((X, Y, Z), 0, 512), ((Y, Z, X), 512, 256), ((Z, X, Y), 768, 256))


def scatter_scratch():
    out = []
    for jobs, lead, rows, pad in ((WO_JOBS, (4,), 48, 16), (WQ_JOBS, (4, 4), 24, 24)):
        for _, _, width in jobs:
            hw = width // 2
            out += [pltpu.VMEM((6,) + lead + (rows, hw), F32), pltpu.VMEM((6,) + lead[1:] + (rows, hw), F32), pltpu.VMEM((3, pad, width), F32),
                    pltpu.VMEM(lead + (rows, width), F32), pltpu.VMEM((4, pad, width), F32)]
    return out


class SmallSums:
    def __init__(self, copies, ar):
        self.c, self.ar = copies, ar
        self.base = copies.slots(10)

    def start(self, n):
        if n < 3:
            for slot, k in enumerate((UP, DOWN, FAR)):
                ref = self.ar.at[n, coord(n)]
                self.c.send(ref, ref, self.base + 3 * n + slot, peer(n, k))
        else:
            ref = self.ar.at[n, lax.axis_index("tp")]
            self.c.send(ref, ref, self.base + 3 * n, partner())

    def finish(self, n):
        ar = self.ar
        if n < 3:
            for slot, k in enumerate((UP, DOWN, FAR)):
                self.c.arrive(ar.at[n, shifted(n, -k)], self.base + 3 * n + slot, peer(n, k))
            total = (ar[n, 0] + ar[n, 1]) + (ar[n, 2] + ar[n, 3])
            ar[n + 1, coord(n + 1) if n < 2 else lax.axis_index("tp")] = total
        else:
            self.c.arrive(ar.at[n, 1 - lax.axis_index("tp")], self.base + 3 * n, partner())


def grads_kernel(o_in, dqkv_in, h_in, dy_in, x_in, wq_in, wo_in, wq2_in, wo2_in, gain_ref, bout_ref, sink_in,
                 y_out, dx_out, gq_out, go_out, gain_out, gbout_out, bqkv_out, sink_out, *scratch):
    bufs = list(scratch)
    o, dqkv, h, dy, x, wq, wo, wq2, wo2, o2, dqkv2, gq, go, ar, loc_sem, send_sem, recv_sem = bufs[:17]
    bufs = bufs[17:]
    tp = lax.axis_index("tp")
    half, d = x.shape
    loads = [pltpu.make_async_copy(a, b, loc_sem.at[n]) for n, (a, b) in enumerate((
        (o_in, o), (dy_in, dy), (h_in, h), (dqkv_in, dqkv), (wo_in, wo), (wo2_in, wo2), (wq_in, wq), (wq2_in, wq2), (x_in, x)))]
    for copy in loads:
        copy.start()
    entry_barrier([peer(dim, k) for dim in range(3) for k in (UP, DOWN, FAR)] + [partner()])
    copies = Copies(send_sem, recv_sem)
    theirs = pl.ds((1 - tp) * half, half)
    slot_x = copies.slots(2)
    copies.send(o_in.at[theirs, :], o2, slot_x, partner())
    copies.send(dqkv_in.at[theirs, :], dqkv2, slot_x + 1, partner())
    small = SmallSums(copies, ar)
    jobs_wo = [scatter_stages(copies, go, go_out, *job, [bufs.pop(0) for _ in range(5)], True) for job in WO_JOBS]
    jobs_wq = [scatter_stages(copies, gq, gq_out, *job, [bufs.pop(0) for _ in range(5)], False) for job in WQ_JOBS]
    own = ar.at[Z, coord(Z)]
    own[...] = jnp.zeros(own.shape, F32)
    for job in jobs_wo:
        s3 = job[2].blk(slice(None))
        s3[...] = jnp.zeros(s3.shape, F32)

    def each(jobs, n, what):
        for job in jobs:
            getattr(job[n], what)()

    loads[0].wait()
    loads[1].wait()

    @pl.loop(0, 2)
    def _(m):
        @pl.loop(0, 3)
        def _(n):
            rows = pl.ds(pl.multiple_of(m * 384, L), 384)
            cols = pl.ds(pl.multiple_of(n * 512, L), 512)
            go[pl.ds(m * 2, 2), :, :, cols] = dot_tn(o[:, rows], dy[:, cols]).reshape(2, 4, 48, 512)

    each(jobs_wo, 0, "start")
    loads[2].wait()
    loads[3].wait()

    @pl.loop(0, 4)
    def _(m):
        gq[m] = dot_tn(h[:, pl.ds(pl.multiple_of(m * 384, L), 384)], dqkv[...]).reshape(4, 4, 24, -1)

    each(jobs_wq, 0, "start")
    ones = jnp.ones((8, 2 * half), BF16)
    own[2:3, 0:dqkv.shape[1]] = jnp.dot(ones, dqkv[...], preferred_element_type=F32)[0:1]
    own[3:4, 0:sink_in.shape[1]] = sink_in[...]
    mine = pl.multiple_of(tp * half, half)
    own[1:2, :] = jnp.dot(ones[:, 0:half], dy[pl.ds(mine, half), :], preferred_element_type=F32)[0:1]
    for copy in loads[4:]:
        copy.wait()
    copies.arrive(o2, slot_x, partner())
    copies.arrive(dqkv2, slot_x + 1, partner())
    each(jobs_wo, 0, "mid")
    tile = half // 3

    @pl.loop(0, 3)
    def _(n):
        at = pl.ds(pl.multiple_of(n * tile, tile), tile)
        at_all = pl.ds(pl.multiple_of(mine + n * tile, tile), tile)
        acc = jnp.dot(o[at_all, :], wo[...], preferred_element_type=F32) + jnp.dot(o2[at, :], wo2[...], preferred_element_type=F32)
        h[at, :] = (x[at, :].astype(F32) + acc + bout_ref[...]).astype(BF16)

    store_y = pltpu.make_async_copy(h.at[pl.ds(0, half), :], y_out, loc_sem.at[0])
    store_y.start()
    each(jobs_wo, 0, "finish")
    each(jobs_wo, 1, "start")
    each(jobs_wq, 0, "mid")
    gain = gain_ref[...]

    @pl.loop(0, 3)
    def _(n):
        at = pl.ds(pl.multiple_of(n * tile, tile), tile)
        at_all = pl.ds(pl.multiple_of(mine + n * tile, tile), tile)
        dh = dot_nt(dqkv[at_all, :], wq[...]) + dot_nt(dqkv2[at, :], wq2[...])
        dh = dh.astype(BF16).astype(F32)
        xv = x[at, :].astype(F32)
        inv = lax.rsqrt(jnp.mean(xv * xv, axis=-1, keepdims=True) + EPS)
        gg = dh * gain
        dx = inv * (gg - xv * (inv * inv * jnp.mean(gg * xv, axis=-1, keepdims=True)))
        dy[at_all, :] = (dy[at_all, :].astype(F32) + dx).astype(BF16)
        own[0:1, :] = own[0:1, :] + jnp.sum(dh * (xv * inv), axis=0, keepdims=True)

    store_dx = pltpu.make_async_copy(dy.at[pl.ds(mine, half), :], dx_out, loc_sem.at[1])
    store_dx.start()
    small.start(0)
    each(jobs_wo, 1, "mid")
    small.finish(0)
    small.start(1)
    each(jobs_wq, 0, "finish")
    each(jobs_wq, 1, "start")
    each(jobs_wo, 1, "finish")
    each(jobs_wo, 2, "start")
    small.finish(1)
    small.start(2)
    each(jobs_wq, 1, "mid")
    small.finish(2)
    small.start(3)
    each(jobs_wo, 2, "finish")
    each(jobs_wq, 1, "finish")
    each(jobs_wq, 2, "start")
    small.finish(3)
    both = ar[3, 0] + ar[3, 1]
    row = ar[3, tp]
    gain_out[...] = both[0:1, :]
    gbout_out[...] = both[1:2, :]
    bqkv_out[...] = row[2:3, 0:bqkv_out.shape[1]]
    lane = lax.broadcasted_iota(jnp.int32, sink_out.shape, 1)
    sinks = jnp.zeros(sink_out.shape, F32)
    for n in range(sink_in.shape[1] // L):
        sinks = jnp.where(lane == n, jnp.sum(row[3:4, n * L:n * L + L], axis=1, keepdims=True), sinks)
    sink_out[...] = sinks
    each(jobs_wq, 2, "finish")
    copies.drain()
    store_y.wait()
    store_dx.wait()


def all_grads(o, dqkv, h, dy, x, wq, wo, wq2, wo2, gain, b_out, sink_part):
    half, d = x.shape
    seq, width = o.shape
    cols = dqkv.shape[1]
    n = 2 + 10 + len(WO_JOBS + WQ_JOBS) * 15
    sds = jax.ShapeDtypeStruct
    row = sds((1, d), F32)
    like = [pltpu.VMEM(a.shape, BF16) for a in (o, dqkv, h, dy, x, wq, wo, wq2, wo2)]
    scratch = like + [pltpu.VMEM((half, width), BF16), pltpu.VMEM((half, cols), BF16), pltpu.VMEM((4, 4, 4, 24, cols), F32), pltpu.VMEM((4, 4, 48, d), F32),
                      pltpu.VMEM((4, 4, 4, d), F32),
                      pltpu.SemaphoreType.DMA((9,)), pltpu.SemaphoreType.DMA((n,)), pltpu.SemaphoreType.DMA((n,))]
    return pl.pallas_call(
        grads_kernel, name="all_grads",
        out_shape=(sds((half, d), BF16), sds((half, d), BF16), sds((24, cols), F32), sds((12, d), F32), row, row, sds((1, cols), F32), sds((1, L), F32)),
        in_specs=[ANY] * 9 + [VM] * 3, out_specs=(ANY, ANY) + (VM,) * 6, scratch_shapes=scratch + scatter_scratch(),
        compiler_params=pltpu.CompilerParams(collective_id=1, has_side_effects=True, vmem_limit_bytes=VMEM_LIMIT),
    )(o, dqkv, h, dy, x, wq, wo, wq2, wo2, gain, b_out, sink_part)


def rope_tables(seq, head_dim):
    inv_freq = ROPE_BASE ** (-2.0 * jnp.arange(head_dim // 2).astype(F32) / head_dim)
    angles = jnp.arange(seq).astype(F32)[:, None] * inv_freq[None, :]
    cos, sin = jnp.cos(angles), jnp.sin(angles)
    return jnp.concatenate([cos, cos], axis=1), jnp.concatenate([-sin, sin], axis=1)


def solution(mesh):
    act_spec = P("fsdp", "tp", None)
    wout_spec = P(("tp", "fsdp"), None)
    in_specs = (act_spec, act_spec, P(), P("fsdp", "tp"), P("tp"), P("tp"), wout_spec, P())
    out_specs = (act_spec, act_spec, P(), P("fsdp", "tp"), P("tp"), P("tp"), wout_spec, P())

    def device_step(resid_loc, grad_loc, norm_gain, wqkv_loc, bqkv_loc, sink_loc, wout_loc, b_out):
        x, dy = resid_loc[0], grad_loc[0]
        half, d = x.shape
        seq = 2 * half
        heads = sink_loc.shape[0]
        width = heads * L
        tp = lax.axis_index("tp")
        wo_slab = jnp.concatenate([wout_loc[:, :d // 2], wout_loc[:, d // 2:]], axis=0)
        wq6, wo6, h_all, dy_all, wq_oth6, wo_oth6 = gather_all(wqkv_loc, wo_slab, x, dy, norm_gain[None, :])

        def wo_rows(w):
            return w.reshape(64, 2, 12, d // 2).transpose(0, 2, 1, 3).reshape(width, d)

        wq, wq_oth = wq6.reshape(d, -1), wq_oth6.reshape(d, -1)
        wo, wo_oth = wo_rows(wo6), wo_rows(wo_oth6)
        h_all, dy_all = h_all.reshape(seq, d), dy_all.reshape(seq, d)
        qkv = (jnp.dot(h_all, wq, preferred_element_type=F32) + bqkv_loc.astype(F32)).astype(BF16)
        d_o = jnp.einsum("tk,hk->th", dy_all, wo, preferred_element_type=F32).astype(BF16)
        cos, sin = rope_tables(seq, 128)
        sink_row = jnp.repeat(sink_loc, 128)[None, :]
        o, dqkv, dsink = attend(qkv, d_o, cos, sin, sink_row)
        outs = all_grads(o, dqkv, h_all, dy_all, x, wq, wo, wq_oth, wo_oth, norm_gain[None, :], b_out.astype(F32)[None, :], dsink)
        resid_out, grad_resid, gq, go, gain_g, bout_g, bqkv_g, sink_g = outs
        return (resid_out[None], grad_resid[None], gain_g[0], gq, bqkv_g[0], sink_g[0, :heads], go, bout_g[0])

    return jax.shard_map(device_step, mesh=mesh, in_specs=in_specs, out_specs=out_specs, check_vma=False)
```

time: 967 us -> 195 us (0.20)
  blocking collectives: 448 us -> 0 us
  matrix products: 189 us -> 11.5 us
  waiting for transfers between devices: 164 us -> 0 us
  Pallas kernels: 0 us -> 143 us
  starting transfers between devices: 51.8 us -> 0 us
  other arithmetic: 40.4 us -> 7.72 us
  local copies, waits for them, and re-layouts: 51.9 us -> 31.7 us
  between operations: 15.5 us -> 0.83 us
    psum x2 -> x0, blocking collectives: 238 us -> none  [the longest x1 175 us: device_step(): grad_bqkv = lax.psum(jnp.sum(d_qkv, axis=(0, 1), dtype=jnp.float32), 'fsdp')]
    unnamed x1 -> x0, blocking collectives: 210 us -> none
    dot_general x90 -> x2, matrix products: 189 us -> 11.5 us  [the longest x1 6.37 us: device_step(): jnp.dot(h_all, wq, preferred_element_type=F32) + bqkv_loc.astype(F32)]
    all_gather x4 -> x0, waiting for transfers between devices: 162 us -> none  [the longest x1 71.1 us: device_step(): wqkv_full = lax.all_gather(wqkv_loc, 'fsdp', axis=0, tiled=True)]
    pallas_call x0 -> x3, Pallas kernels: none -> 143 us  [the longest x1 69.1 us: all_grads(): pl.pallas_call(grads_kernel, name='all_grads', out_shape=(sds((half, d),...]
    unnamed x16 -> x0, starting transfers between devices: 51.5 us -> none
    unnamed x66 -> x35, local copies, waits for them, and re-layouts: 39.3 us -> 9.65 us
    reduce_sum x28 -> x0, other arithmetic: 15.6 us -> none  [the longest x1 7.13 us: device_step(): jnp.sum(grad_loc, axis=(0, 1), dtype=jnp.float32)]
  transfers between devices with their start and end apart: 23 -> 0, of which waited for: 4 -> 0; matrix products, arithmetic and copies ran while one was open for 31% -> 0% of each run, Pallas kernels for 0% -> 0%
where the time goes in v1:
time: 195 us
  Pallas kernels  143 us (73%)
  local copies, waits for them, and re-layouts  31.7 us (16%)
  matrix products  11.5 us (6%)
  other arithmetic  7.72 us (4%)
    pallas_call x1, Pallas kernels, all_grads(): pl.pallas_call(grads_kernel, name='all_grads', out_shape=(sds((half, d),...  69.1 us
    pallas_call x1, Pallas kernels, gather_all(): pl.pallas_call(gather_kernel, name='gather_all', out_shape=(wq_shape, wo_...  52.1 us
    pallas_call x1, Pallas kernels, attend(): pl.pallas_call(kernel, name='attend', grid=(n_blocks,), out_shape=(jax.Sh...  22.1 us
    unnamed x35, local copies, waits for them, and re-layouts  9.65 us
    transpose x2, local copies, waits for them, and re-layouts, wo_rows(): return w.reshape(64, 2, 12, d // 2).transpose(0, 2, 1, 3).reshape(width, d)  8.33 us
    dot_general x1, matrix products, device_step(): jnp.dot(h_all, wq, preferred_element_type=F32) + bqkv_loc.astype(F32)  6.37 us
    pallas_call x2, local copies, waits for them, and re-layouts, gather_all(): pl.pallas_call(gather_kernel, name='gather_all', out_shape=(wq_shape, wo_...  5.75 us
    dot_general x1, matrix products, device_step(): jnp.einsum('tk,hk->th', dy_all, wo, preferred_element_type=F32).astype(BF16)  5.1 us

profile of v1, /device:TPU:0, one launch (start us, length us, event | category | flops | bytes accessed | tf_op | source)
XLA Modules:
  0.0 195.0 jit_solution(8572747679785003626)
XLA Ops:
  0.6 0.8 fusion.1
  1.4 0.6 pad_maximum_fusion.2.wo_in
  2.0 1.3 broadcast_in_dim.21.g_ref.gain_ref
  3.3 52.1 %gather_all.1 = (bf16[4,4,4,24,1024]{4,3,2,1,0:T(8,128)(2,1)}, bf16[4,4,4,24,768]{4,3,2,1,0:T(8,128)(2,1)}, bf16[2,768,1536]{2,1,0:T(8,128)(2,1)}, bf16[2,768,15...) custom-call(bf16[24,1024]{1,0:T(8,128)(2,1)} %wq_in.1, ...), custom_call_target="tpu_custom_call" | custom-call | tf_op jit(solution)/shard_map/gather_all/pallas_call | solution.py:204
  55.4 2.9 %copy.18 = bf16[4,4,4,24,768]{4,2,1,0,3:T(4,128)(2,1)S(1)} copy(bf16[4,4,4,24,768]{4,3,2,1,0:T(8,128)(2,1)} %get-tuple-element.28) | data formatting | bytes 4718592 | tf_op jit(solution)/shard_map/gather_all/pallas_call | solution.py:204
  58.3 2.1 %reshape.54 = bf16[64,2,12,768]{3,0,2,1:T(8,128)(2,1)} reshape(bf16[4,4,4,24,768]{4,2,1,0,3:T(4,128)(2,1)S(1)} %copy.18) | data formatting | bytes 4718592 | tf_op jit(solution)/shard_map/reshape | solution.py:637
  60.4 4.2 %copy.19 = bf16[64,12,2,768]{3,2,1,0:T(2,128)(2,1)S(1)} copy(bf16[64,12,2,768]{3,0,1,2:T(8,128)(2,1)} %bitcast.33) | data formatting | bytes 4718592 | tf_op jit(solution)/shard_map/transpose | solution.py:637
  65.2 5.1 %convolution_convert_fusion.refs_1_ = bf16[1536,768]{1,0:T(8,128)(2,1)} fusion(bf16[1536,1536]{1,0:T(8,128)(2,1)S(1)} %bitcast.49, bf16[768,1536]{1,0:T(8,128)(2,1)S(1)} %bitcast.39), kind=kOutput, calls=%fused_computation.1 | convolution fusion | flops 3625058304 | bytes 9437184 | tf_op jit(solution)/shard_map/tk,hk->th/dot_general | solution.py:643
  70.4 6.4 %add_convert_fusion.refs_0_ = bf16[1536,1024]{1,0:T(8,128)(2,1)} fusion(bf16[1536,1536]{1,0:T(8,128)(2,1)S(1)} %bitcast.45, bf16[1536,1024]{1,0:T(8,128)(2,1)S(1)} %bitcast.51, f32[1024]{0:T(1024)S(1)} %convert_element_type.36), kind=kOutput, calls=%fused_computation | convolution fusion | flops 4834983936 | bytes 11014144 | tf_op jit(solution)/shard_map/dot_general | solution.py:642
  76.7 2.8 %fusion = (f32[1536,64]{1,0:T(8,128)S(1)}, f32[1536,64]{1,0:T(8,128)S(1)}, f32[1536,64]{1,0:T(8,128)S(1)}) fusion(f32[64]{0:T(128)S(1)} %multiply_power_fusion, f32[1536]{0:T(1024)S(1)} %iota_convert_fusion), kind=kLoop, calls=%fused_computation.6 | loop fusion | flops 196608 | bytes 1186048 | tf_op jit(solution)/shard_map/neg | solution.py:617
  79.6 1.6 pad_maximum_fusion
  81.9 22.1 %attend.1 = (bf16[1536,768]{1,0:T(8,128)(2,1)}, bf16[1536,1024]{1,0:T(8,128)(2,1)}, f32[1,768]{1,0:T(1,128)}) custom-call(bf16[1536,1024]{1,0:T(8,128)(2,1)} %add_convert_fusion.refs_0_, bf16[1536,768]{1,0:T(8,128)(2,1)} %convolution_convert_fusion.refs_1_, f32[1536,128]{1,0:T(8,128)} %get-tuple-element.47.refs_2_, f32[1536,128]{1,0:T(8,128)} %get-tuple-element.48.refs_3_, ...), custom_call_target="tpu_custom_call" | custom-call | tf_op jit(solution)/shard_map/attend/pallas_call | solution.py:321
  104.0 2.9 %copy.20 = bf16[4,4,4,24,768]{4,2,1,0,3:T(4,128)(2,1)S(1)} copy(bf16[4,4,4,24,768]{4,3,2,1,0:T(8,128)(2,1)} %get-tuple-element.32) | data formatting | bytes 4718592 | tf_op jit(solution)/shard_map/gather_all/pallas_call | solution.py:204
  106.8 2.1 %reshape.57 = bf16[64,2,12,768]{3,0,2,1:T(8,128)(2,1)} reshape(bf16[4,4,4,24,768]{4,2,1,0,3:T(4,128)(2,1)S(1)} %copy.20) | data formatting | bytes 4718592 | tf_op jit(solution)/shard_map/reshape | solution.py:637
  109.0 4.1 %copy.21 = bf16[64,12,2,768]{3,2,1,0:T(2,128)(2,1)S(1)} copy(bf16[64,12,2,768]{3,0,1,2:T(8,128)(2,1)} %bitcast.35) | data formatting | bytes 4718592 | tf_op jit(solution)/shard_map/transpose | solution.py:637
  113.1 1.8 copy.24
  115.5 69.1 %all_grads.1 = (bf16[768,1536]{1,0:T(8,128)(2,1)}, bf16[768,1536]{1,0:T(8,128)(2,1)}, f32[24,1024]{1,0:T(8,128)}, f32[12,1536]{1,0:T(8,128)}, f32[1,1536]{1,0:T(...) custom-call(bf16[1536,768]{1,0:T(8,128)(2,1)} %get-tuple-element.29.o_in, ...), custom_call_target="tpu_custom_call" | custom-call | tf_op jit(solution)/shard_map/all_grads/pallas_call | solution.py:605
  184.6 1.3 reduce
  185.9 1.3 reduce.1
  187.2 1.1 slice_bitcast_fusion
  188.4 3.4 %copy.32 = bf16[1,768,1536]{2,1,0:T(8,128)(2,1)} copy(bf16[1,768,1536]{2,1,0:T(8,128)(2,1)} %bitcast.55) | data formatting | bytes 4718592
  191.7 1.4 copy.33
  193.2 0.6 copy.34
  194.4 0.6 copy.36
  (36 shorter events, 2.4 us)
Async XLA Ops:
  0.6 80.6 %copy-start = (f32[6]{0:T(128)S(1)}, f32[6]{0:T(128)}, u32[]{:S(2)}) copy-start(f32[6]{0:T(128)} %param.13) | copy-start | bytes 76
  58.3 6.8 %slice-start.2 = ((s8[4718592]{0:T(1024)(128)(4,1)}), s8[524288]{0:T(1024)(128)(4,1)S(1)}, s32[]{:S(2)}) async-start(s8[4718592]{0:T(1024)(128)(4,1)} %bitcast.47), calls=%async_computation.2 | async-start | bytes 1048576
  60.4 4.7 %slice-start.3 = ((s8[4718592]{0:T(1024)(128)(4,1)}), s8[4194304]{0:T(1024)(128)(4,1)S(1)}, s32[]{:S(2)}) async-start(s8[4718592]{0:T(1024)(128)(4,1)} %bitcast.47), calls=%async_computation.3 | async-start | bytes 8388608
  64.7 5.6 %slice-start = ((s8[4718592]{0:T(1024)(128)(4,1)}), s8[4194304]{0:T(1024)(128)(4,1)S(1)}, s32[]{:S(2)}) async-start(s8[4718592]{0:T(1024)(128)(4,1)} %bitcast.43), calls=%async_computation | async-start | bytes 8388608
  65.1 5.2 %copy-start.1 = (bf16[96,8,2,768]{3,1,2,0:T(8,128)(2,1)}, bf16[96,8,2,768]{3,1,2,0:T(8,128)(2,1)S(1)}, u32[]{:S(2)}) copy-start(bf16[96,8,2,768]{3,1,2,0:T(8,128)(2,1)S(1)} %copy.22) | copy-start | bytes 7077892
  65.2 5.1 %copy-start.8 = (bf16[1024]{0:T(1024)(128)(2,1)S(1)}, bf16[1024]{0:T(1024)(128)(2,1)}, u32[]{:S(2)}) copy-start(bf16[1024]{0:T(1024)(128)(2,1)} %param.12) | copy-start | bytes 6148
  65.2 5.1 %slice-start.1 = ((s8[4718592]{0:T(1024)(128)(4,1)}), s8[524288]{0:T(1024)(128)(4,1)S(1)}, s32[]{:S(2)}) async-start(s8[4718592]{0:T(1024)(128)(4,1)} %bitcast.43), calls=%async_computation.1 | async-start | bytes 1048576
  65.2 5.1 %copy-start.2 = (bf16[4,4,4,24,1024]{4,3,2,1,0:T(8,128)(2,1)S(1)}, bf16[4,4,4,24,1024]{4,3,2,1,0:T(8,128)(2,1)}, u32[]{:S(2)}) copy-start(bf16[4,4,4,24,1024]{4,3,2,1,0:T(8,128)(2,1)} %get-tuple-element.26) | copy-start | bytes 9437188
  113.1 1.9 copy-start.6
  188.4 3.4 %copy-start.3 = (bf16[768,1536]{1,0:T(8,128)(2,1)S(1)}, bf16[768,1536]{1,0:T(8,128)(2,1)}, u32[]{:S(2)}) copy-start(bf16[768,1536]{1,0:T(8,128)(2,1)} %get-tuple-element.35) | copy-start | bytes 7077892
  191.7 1.4 copy-start.5
  191.7 2.1 %copy-start.7 = (f32[1,1024]{1,0:T(1,128)S(1)}, f32[1,1024]{1,0:T(1,128)}, u32[]{:S(2)}) copy-start(f32[1,1024]{1,0:T(1,128)} %get-tuple-element.38) | copy-start | bytes 12292
  191.7 2.7 %copy-start.4 = (f32[12,1536]{1,0:T(8,128)S(1)}, f32[12,1536]{1,0:T(8,128)}, u32[]{:S(2)}) copy-start(f32[12,1536]{1,0:T(8,128)} %get-tuple-element.63) | copy-start | bytes 221188

commit v2 on v1

v2 whole, which is shorter than its diff:
```python
import jax
import jax.numpy as jnp
import numpy as np
from jax import lax
from jax.experimental import pallas as pl
from jax.experimental.pallas import tpu as pltpu
from jax.sharding import PartitionSpec as P

EPS = 1e-5
ROPE_BASE = 150000.0
WINDOW = 128
MESH = pl.DeviceIdType.MESH
STRIDE = (16, 4, 1)
F32 = jnp.float32
BF16 = jnp.bfloat16
VMEM_LIMIT = 67_000_000
Z, Y, X = range(3)
UP, DOWN, FAR = 1, -1, 2
L = 128
NEG = -1e30


def coord(dim):
    return lax.rem(lax.div(lax.axis_index("fsdp"), STRIDE[dim]), 4)


def shifted(dim, k):
    return lax.rem(coord(dim) + (k + 4), 4)


def peer(dim, k):
    f = lax.axis_index("fsdp")
    return {"fsdp": f + (shifted(dim, k) - coord(dim)) * STRIDE[dim]}


def partner():
    return {"tp": 1 - lax.axis_index("tp")}


def entry_barrier(peers):
    barrier = pltpu.get_barrier_semaphore()
    for p in peers:
        pl.semaphore_signal(barrier, inc=1, device_id=p, device_id_type=MESH)
    pl.semaphore_wait(barrier, len(peers))


class Copies:
    def __init__(self, send_sem, recv_sem):
        self.send_sem, self.recv_sem = send_sem, recv_sem
        self.n = 0
        self.sent = []

    def slots(self, count):
        first = self.n
        self.n += count
        return first

    def make(self, src, dst, slot, device):
        return pltpu.make_async_remote_copy(src_ref=src, dst_ref=dst, send_sem=self.send_sem.at[slot], recv_sem=self.recv_sem.at[slot], device_id=device, device_id_type=MESH)

    def send(self, src, dst, slot, device):
        copy = self.make(src, dst, slot, device)
        copy.start()
        self.sent.append(copy)

    def arrive(self, ref, slot, device):
        self.make(ref, ref, slot, device).wait_recv()

    def drain(self):
        for copy in self.sent:
            copy.wait_send()
        self.sent = []


class GatherStage:
    def __init__(self, copies, dim, slot_view, own_view):
        self.c, self.dim, self.view, self.own = copies, dim, slot_view, own_view
        self.base = copies.slots(6)

    def start(self):
        me = coord(self.dim)
        for h in (0, 1):
            self.c.send(self.own(h), self.view(me, h), self.base + h, peer(self.dim, UP))
            self.c.send(self.own(1 - h), self.view(me, 1 - h), self.base + 3 - h, peer(self.dim, DOWN))

    def sides(self):
        return [(shifted(self.dim, k), peer(self.dim, k)) for k in (DOWN, UP)]

    def mid(self):
        (lo, down), (hi, up) = self.sides()
        self.c.arrive(self.view(lo, 0), self.base, down)
        self.c.send(self.view(lo, 0), self.view(lo, 0), self.base + 4, up)
        self.c.arrive(self.view(hi, 1), self.base + 3, up)
        self.c.send(self.view(hi, 1), self.view(hi, 1), self.base + 5, down)

    def finish(self):
        (lo, down), (hi, up) = self.sides()
        far = shifted(self.dim, FAR)
        for n, (at, h, dev) in enumerate(((lo, 1, down), (hi, 0, up))):
            self.c.arrive(self.view(at, h), self.base + 1 + n, dev)
            self.c.arrive(self.view(far, n), self.base + 4 + n, dev)


class GatherDirect:
    def __init__(self, copies, dim, view, own):
        self.c, self.dim, self.view, self.own = copies, dim, view, own
        self.base = copies.slots(3)

    def start(self):
        for slot, k in enumerate((UP, DOWN, FAR)):
            self.c.send(self.own(), self.view(coord(self.dim)), self.base + slot, peer(self.dim, k))

    def finish(self):
        for slot, k in enumerate((UP, DOWN, FAR)):
            self.c.arrive(self.view(shifted(self.dim, -k)), self.base + slot, peer(self.dim, k))


def gather_stages(copies, in_ref, out_ref, order, first, widths):
    whole = pl.ds(first, sum(widths))
    halves = [pl.ds(first, widths[0]), pl.ds(first + widths[0], widths[1])]

    def view(n, c, cols):
        idx = [coord(dim) for dim in range(3)]
        for dim in order[:n]:
            idx[dim] = slice(None)
        idx[order[n]] = c
        return out_ref.at[tuple(idx) + (slice(None), cols)]

    return (GatherDirect(copies, order[0], lambda c: view(0, c, whole), lambda: in_ref.at[:, whole]),
            GatherDirect(copies, order[1], lambda c: view(1, c, whole), lambda: view(1, coord(order[1]), whole)),
            GatherStage(copies, order[2], lambda c, h: view(2, c, halves[h]), lambda h: view(2, coord(order[2]), halves[h])))


ORDERS = ((X, Y, Z), (Y, Z, X), (Z, X, Y))
WQ_GATHER = ((0, (256, L)), (384, (L, 256)), (768, (L, L)))
WO_GATHER = ((0, (L, L)), (256, (L, L)), (512, (L, L)))


def rotate(vals, cos, sin):
    return vals * cos + pltpu.roll(vals, L // 2, 1) * sin


def stack_heads(vals):
    return jnp.concatenate([vals[:, n:n + L] for n in range(0, vals.shape[1], L)], axis=0)


def unstack_heads(vals):
    return jnp.concatenate([vals[n:n + L, :] for n in range(0, vals.shape[0], L)], axis=1)


def dot_nn(a, b):
    return jnp.dot(a, b, preferred_element_type=F32)


def dot_tn(a, b):
    return lax.dot_general(a, b, (((0,), (0,)), ((), ())), preferred_element_type=F32)


def dot_nt(a, b):
    return lax.dot_general(a, b, (((1,), (1,)), ((), ())), preferred_element_type=F32)


def attend(qkv, o, tab_ref, base_ref, sink, dsink, k_buf, v_buf, dk_buf, dv_buf):
    width = o.shape[1]
    heads = width // L
    n_blocks = o.shape[0] // L
    scale = L ** -0.5
    low, high = pl.ds(0, L), pl.ds(L, L)
    k_cols, v_cols = pl.ds(width, L), pl.ds(width + L, L)
    for buf in (k_buf, v_buf, dk_buf, dv_buf, dsink):
        buf[...] = jnp.zeros(buf.shape, buf.dtype)

    def tables(i):
        cos_b, sin_b = base_ref[0, pl.ds(i, 1), :], base_ref[1, pl.ds(i, 1), :]
        cos_r, sin_r = tab_ref[0], tab_ref[1]
        return cos_b * cos_r - sin_b * sin_r, sin_b * cos_r + cos_b * sin_r

    def put_kv(i, dk, dv):
        cos, sin = tables(i)
        at = pl.ds(pl.multiple_of(i * L, L), L)
        qkv[at, k_cols] = rotate(dk.astype(BF16).astype(F32), cos, -sin).astype(BF16)
        qkv[at, v_cols] = dv.astype(BF16)

    @pl.loop(0, n_blocks)
    def _(i):
        for buf in (k_buf, v_buf, dk_buf, dv_buf):
            buf[low, :] = buf[high, :]
        at = pl.ds(pl.multiple_of(i * L, L), L)
        cos, sin = tables(i)
        cos_all = jnp.concatenate([cos] * heads, axis=0)
        sin_all = jnp.concatenate([sin] * heads, axis=0)
        k_buf[high, :] = rotate(qkv[at, k_cols].astype(F32), cos, sin).astype(BF16)
        v_buf[high, :] = qkv[at, v_cols]
        q = rotate(stack_heads(qkv[at, pl.ds(0, width)]).astype(F32), cos_all, sin_all).astype(BF16)
        do = stack_heads(o[at, :])
        keys, vals = k_buf[...], v_buf[...]
        k_idx = lax.broadcasted_iota(jnp.int32, (2 * L, L), 0)
        q_idx = lax.broadcasted_iota(jnp.int32, (2 * L, L), 1)
        allowed = (k_idx > q_idx) & (k_idx <= q_idx + WINDOW) & ((k_idx >= WINDOW) | (i > 0))
        bias = jnp.where(allowed, 0.0, NEG)
        scores = dot_nt(keys, q) * scale + jnp.concatenate([bias] * heads, axis=1)
        top = jnp.maximum(jnp.max(scores, axis=0, keepdims=True), sink)
        probs = jnp.exp(scores - top)
        sink_exp = jnp.exp(sink - top)
        inv = 1.0 / (jnp.sum(probs, axis=0, keepdims=True) + sink_exp)
        probs = probs * inv
        probs_b = probs.astype(BF16)
        o[at, :] = unstack_heads(dot_tn(probs_b, vals).astype(BF16))
        d_probs = dot_nt(vals, do).astype(BF16).astype(F32)
        row_dot = jnp.sum(probs * d_probs, axis=0, keepdims=True)
        d_scores = (probs * (d_probs - row_dot)).astype(BF16)
        dsink[...] = dsink[...] - sink_exp * inv * row_dot
        for buf, new in ((dv_buf, dot_nn(probs_b, do)), (dk_buf, dot_nn(d_scores, q) * scale)):
            buf[low, :] = buf[low, :] + new[0:L, :]
            buf[high, :] = new[L:, :]
        dq = (dot_tn(d_scores, keys) * scale).astype(BF16).astype(F32)
        qkv[at, pl.ds(0, width)] = unstack_heads(rotate(dq, cos_all, -sin_all).astype(BF16))

        @pl.when(i > 0)
        def _():
            put_kv(i - 1, dk_buf[low, :], dv_buf[low, :])

    put_kv(n_blocks - 1, dk_buf[high, :], dv_buf[high, :])


class ScatterStage:
    def __init__(self, copies, dim, blk, buf, put):
        self.c, self.dim, self.blk, self.buf, self.put = copies, dim, blk, buf, put
        self.base = copies.slots(6)
        self.a_up, self.a_down, self.lo = 0, 1, (2, 3)
        self.hi = (4, 5)

    def send(self, src, slot, k):
        self.c.send(src, self.buf.at[slot], self.base + slot, peer(self.dim, k))

    def arrive(self, slot, k):
        self.c.arrive(self.buf.at[slot], self.base + slot, peer(self.dim, k))

    def start(self):
        up, down, far = (shifted(self.dim, k) for k in (UP, DOWN, FAR))
        self.send(self.blk(far, 0), self.a_up, UP)
        self.send(self.blk(far, 1), self.a_down, DOWN)
        self.send(self.blk(up, 1), self.lo[1], UP)
        self.send(self.blk(down, 0), self.hi[0], DOWN)

    def add(self, slot, src):
        dst = self.buf.at[slot]
        if len(src.shape) == 2:
            dst[...] = dst[...] + src[...]
        else:
            @pl.loop(0, src.shape[0])
            def _(j):
                dst[j] = dst[j] + src[j]

    def mid(self):
        self.arrive(self.a_up, DOWN)
        self.add(self.a_up, self.blk(shifted(self.dim, UP), 0))
        self.arrive(self.a_down, UP)
        self.add(self.a_down, self.blk(shifted(self.dim, DOWN), 1))
        self.send(self.buf.at[self.a_up], self.lo[0], UP)
        self.send(self.buf.at[self.a_down], self.hi[1], DOWN)

    def finish(self):
        me = coord(self.dim)
        for h in (1, 0):
            self.arrive(self.lo[h], DOWN)
            self.arrive(self.hi[1 - h], UP)
        for h in (0, 1):
            own, a, b = self.blk(me, h), self.buf.at[self.lo[h]], self.buf.at[self.hi[h]]
            if len(own.shape) == 2:
                self.put(h, None, own[...] + a[...] + b[...])
            else:
                @pl.loop(0, own.shape[0])
                def _(j):
                    self.put(h, j, own[j] + a[j] + b[j])


class DirectStage:
    def __init__(self, copies, dim, blk, buf, put):
        self.c, self.dim, self.blk, self.buf, self.put = copies, dim, blk, buf, put
        self.base = copies.slots(3)

    def start(self):
        for slot, k in enumerate((UP, DOWN, FAR)):
            self.c.send(self.blk(shifted(self.dim, k)), self.buf.at[slot], self.base + slot, peer(self.dim, k))

    def finish(self):
        for slot, k in enumerate((UP, DOWN, FAR)):
            self.c.arrive(self.buf.at[slot], self.base + slot, peer(self.dim, k))
        b = self.buf
        self.put((self.blk(coord(self.dim))[...] + b[0]) + (b[1] + b[2]))


def scatter_stages(copies, src, out, order, first, width, bufs, padded):
    hw = width // 2
    r1, r2, r3, s2, s3 = bufs
    rows = out.shape[0]
    rest = [dim for dim in range(3) if dim != order[0]]

    def pick(ref, at, t, cols):
        idx = [slice(None)] * (len(ref.shape) - 1)
        idx[at] = t
        return ref.at[tuple(idx) + (cols,)]

    def part(h, base=0):
        return pl.ds(base + h * hw, hw)

    def put1(h, j, val):
        s2[j, ..., part(h)] = val

    def put2(h, j, val):
        if padded:
            for t in range(4):
                s3[t, 0:rows, part(h)] = val[rows * t:rows * t + rows, :]
        else:
            s3[j, :, part(h)] = val

    def put3(val):
        out[:, pl.ds(first, width)] = val[0:rows, :]

    return (ScatterStage(copies, order[0], lambda t, h: pick(src, order[0], t, part(h, first)), r1, put1),
            ScatterStage(copies, order[1], lambda t, h: pick(s2, rest.index(order[1]), t, part(h)), r2, put2),
            DirectStage(copies, order[2], lambda t: s3.at[t], r3, put3))


WO_JOBS = (((Y, Z, X), 0, 768), ((Z, Y, X), 768, 768))
WQ_JOBS = (((X, Y, Z), 0, 512), ((Y, Z, X), 512, 256), ((Z, X, Y), 768, 256))


def scatter_scratch():
    out = []
    for jobs, lead, rows, pad in ((WO_JOBS, (4,), 48, 16), (WQ_JOBS, (4, 4), 24, 24)):
        for _, _, width in jobs:
            hw = width // 2
            out += [pltpu.VMEM((6,) + lead + (rows, hw), F32), pltpu.VMEM((6,) + lead[1:] + (rows, hw), F32), pltpu.VMEM((3, pad, width), F32),
                    pltpu.VMEM(lead + (rows, width), F32), pltpu.VMEM((4, pad, width), F32)]
    return out


class SmallSums:
    def __init__(self, copies, ar):
        self.c, self.ar = copies, ar
        self.base = copies.slots(10)

    def start(self, n):
        if n < 3:
            for slot, k in enumerate((UP, DOWN, FAR)):
                ref = self.ar.at[n, coord(n)]
                self.c.send(ref, ref, self.base + 3 * n + slot, peer(n, k))
        else:
            ref = self.ar.at[n, lax.axis_index("tp")]
            self.c.send(ref, ref, self.base + 3 * n, partner())

    def finish(self, n):
        ar = self.ar
        if n < 3:
            for slot, k in enumerate((UP, DOWN, FAR)):
                self.c.arrive(ar.at[n, shifted(n, -k)], self.base + 3 * n + slot, peer(n, k))
            total = (ar[n, 0] + ar[n, 1]) + (ar[n, 2] + ar[n, 3])
            ar[n + 1, coord(n + 1) if n < 2 else lax.axis_index("tp")] = total
        else:
            self.c.arrive(ar.at[n, 1 - lax.axis_index("tp")], self.base + 3 * n, partner())


def layer_kernel(wq_in, wo_in, x_in, x5_in, dy_in, small_in, perm_ref, tab_ref, base_ref,
                 y_out, dx_out, gq_out, go_out, gain_out, gbout_out, bqkv_out, sink_out, *scratch):
    bufs = list(scratch)
    (wq5, wo5, h, dy, qkv, o, wq, wo, wq2, wo2, o2, dqkv2, gq, go, ar, k_buf, v_buf, dk_buf, dv_buf, dsink,
     loc_sem, send_sem, recv_sem) = bufs[:23]
    bufs = bufs[23:]
    tp = lax.axis_index("tp")
    half, d = x_in.shape
    width, cols = o.shape[1], qkv.shape[1]
    start = pl.multiple_of(tp * half, half)
    mine, theirs = pl.ds(start, half), pl.ds((1 - tp) * half, half)
    wide, rest = pl.ds(0, cols), pl.ds(0, d - cols)
    x_low, x_high = qkv.at[pl.ds(0, half), :], qkv.at[pl.ds(half, half), rest]
    local = [pltpu.make_async_copy(a, b, loc_sem.at[n]) for n, (a, b) in enumerate((
        (x_in.at[:, wide], x_low), (x_in.at[:, pl.ds(cols, d - cols)], x_high), (dy_in, dy.at[mine, :])))]
    for copy in local:
        copy.start()
    for ref, own in ((wq5, wq_in), (wo5, wo_in)):
        ref[coord(Z), coord(Y), coord(X)] = own[...]
    entry_barrier([peer(dim, k) for dim in range(3) for k in (UP, DOWN, FAR)] + [partner()])
    copies = Copies(send_sem, recv_sem)
    jobs_q = [gather_stages(copies, wq_in, wq5, order, *job) for order, job in zip(ORDERS, WQ_GATHER)]
    jobs_o = [gather_stages(copies, wo_in, wo5, order, *job) for order, job in zip(ORDERS, WO_GATHER)]

    def each(jobs, n, *names):
        for name in names:
            for job in jobs:
                getattr(job[n], name)()

    each(jobs_q, 0, "start")
    each(jobs_o, 0, "start")
    gain, b_out = small_in[0:1, :], small_in[1:2, :]
    parts = 6
    step = half // parts
    slot_h, slot_dy = copies.slots(parts), copies.slots(5)
    for copy in local:
        copy.wait()
    copies.send(dy.at[mine, :], dy.at[mine, :], slot_dy, partner())

    def norm_part(k):
        @pl.loop(0, step // 32)
        def _(i):
            n = k * step + i * 32
            at = pl.ds(pl.multiple_of(n, 32), 32)
            xv = jnp.concatenate([x_low[at, :], x_high[at, :]], axis=1).astype(F32)
            inv = lax.rsqrt(jnp.mean(xv * xv, axis=-1, keepdims=True) + EPS)
            h[pl.ds(pl.multiple_of(start + n, 32), 32), :] = (xv * inv * gain).astype(BF16)

    def send_part(k):
        at = pl.ds(pl.multiple_of(start + k * step, step), step)
        copies.send(h.at[at, :], h.at[at, :], slot_h + k, partner())

    norm_part(0)
    norm_part(1)
    each(jobs_q, 0, "finish")
    each(jobs_q, 1, "start")
    each(jobs_o, 0, "finish")
    send_part(0)
    send_part(1)
    norm_part(2)
    norm_part(3)
    each(jobs_q, 1, "finish")
    each(jobs_q, 2, "start")
    each(jobs_o, 1, "start")
    send_part(2)
    send_part(3)
    norm_part(4)
    norm_part(5)
    each(jobs_o, 1, "finish")
    send_part(4)
    send_part(5)
    each(jobs_q, 2, "mid")
    each(jobs_o, 2, "start")
    for k in range(parts):
        copies.arrive(h.at[pl.ds((1 - tp) * half + k * step, step), :], slot_h + k, partner())
    copies.arrive(dy.at[theirs, :], slot_dy, partner())
    each(jobs_q, 2, "finish")

    @pl.loop(0, 16)
    def _(n):
        wq[pl.ds(pl.multiple_of(n * 96, 32), 96), :] = wq5[lax.div(n, 4), lax.rem(n, 4)].reshape(96, cols)

    copies.send(wq, wq2, slot_dy + 1, partner())
    bias = small_in[2:3, 0:cols]
    tile = 512

    def qkv_tile(n):
        qkv[pl.ds(n * tile, tile), :] = (dot_nn(h[pl.ds(n * tile, tile), :], wq[...]) + bias).astype(BF16)

    qkv_tile(0)
    qkv_tile(1)
    each(jobs_o, 2, "mid")
    qkv_tile(2)
    each(jobs_o, 2, "finish")

    def slabs(z, pair):
        return wo5[z, pl.ds(pair * 2, 2)].reshape(192, d // 2)

    @pl.loop(0, 8)
    def _(n):
        group = slabs(lax.div(n, 2), lax.rem(n, 2))
        for c in (0, 1):
            wo[pl.ds(pl.multiple_of(n * 96, 32), 96), pl.ds(c * (d // 2), d // 2)] = dot_nn(perm_ref[c], group).astype(BF16)

    @pl.loop(0, 3)
    def _(n):
        at = pl.ds(pl.multiple_of(n * tile, tile), tile)
        o[at, :] = dot_nt(dy[at, :], wo[...]).astype(BF16)

    copies.send(wo, wo2, slot_dy + 2, partner())
    attend(qkv, o, tab_ref, base_ref, small_in[3:4, 0:width], dsink, k_buf, v_buf, dk_buf, dv_buf)
    copies.arrive(wq2, slot_dy + 1, partner())
    copies.arrive(wo2, slot_dy + 2, partner())
    copies.drain()
    copies.send(o.at[theirs, :], o2, slot_dy + 3, partner())
    copies.send(qkv.at[theirs, :], dqkv2, slot_dy + 4, partner())
    loads = [pltpu.make_async_copy(x5_in.at[:, :, :, :, pl.ds(c * (d // 2), d // 2)], wo5.at[pl.ds(c * 2, 2)], loc_sem.at[c]) for c in (0, 1)]
    for copy in loads:
        copy.start()

    small = SmallSums(copies, ar)
    jobs_wo = [scatter_stages(copies, go, go_out, *job, [bufs.pop(0) for _ in range(5)], True) for job in WO_JOBS]
    jobs_wq = [scatter_stages(copies, gq, gq_out, *job, [bufs.pop(0) for _ in range(5)], False) for job in WQ_JOBS]
    own = ar.at[Z, coord(Z)]
    own[...] = jnp.zeros(own.shape, F32)
    for job in jobs_wo:
        s3 = job[2].blk(slice(None))
        s3[...] = jnp.zeros(s3.shape, F32)

    @pl.loop(0, 2)
    def _(m):
        @pl.loop(0, 3)
        def _(n):
            at, to = pl.ds(pl.multiple_of(m * 384, L), 384), pl.ds(pl.multiple_of(n * tile, L), tile)
            go[pl.ds(m * 2, 2), :, :, to] = dot_tn(o[:, at], dy[:, to]).reshape(2, 4, 48, tile)

    each(jobs_wo, 0, "start")

    @pl.loop(0, 4)
    def _(m):
        gq[m] = dot_tn(h[:, pl.ds(pl.multiple_of(m * 384, L), 384)], qkv[...]).reshape(4, 4, 24, cols)

    each(jobs_wq, 0, "start")
    ones = jnp.ones((8, 2 * half), BF16)
    own[2:3, 0:cols] = dot_nn(ones, qkv[...])[0:1]
    own[3:4, 0:width] = dsink[...]
    own[1:2, :] = dot_nn(ones[:, 0:half], dy[mine, :])[0:1]
    for copy in loads:
        copy.wait()
    copies.arrive(o2, slot_dy + 3, partner())
    copies.arrive(dqkv2, slot_dy + 4, partner())
    each(jobs_wo, 0, "mid")
    third = 192

    def x_tile(n):
        return jnp.concatenate([slabs(lax.div(n, 2) + c, lax.rem(n, 2)) for c in (0, 2)], axis=1).astype(F32)

    @pl.loop(0, 4)
    def _(n):
        at = pl.ds(pl.multiple_of(n * third, third), third)
        at_all = pl.ds(pl.multiple_of(start + n * third, third), third)
        acc = dot_nn(o[at_all, :], wo[...]) + dot_nn(o2[at, :], wo2[...])
        h[at, :] = (x_tile(n) + acc + b_out).astype(BF16)

    store_y = pltpu.make_async_copy(h.at[pl.ds(0, half), :], y_out, loc_sem.at[0])
    store_y.start()
    each(jobs_wo, 0, "finish")
    each(jobs_wo, 1, "start")
    each(jobs_wq, 0, "mid")

    @pl.loop(0, 4)
    def _(n):
        at = pl.ds(pl.multiple_of(n * third, third), third)
        at_all = pl.ds(pl.multiple_of(start + n * third, third), third)
        dh = dot_nt(qkv[at_all, :], wq[...]) + dot_nt(dqkv2[at, :], wq2[...])
        dh = dh.astype(BF16).astype(F32)
        xv = x_tile(n)
        inv = lax.rsqrt(jnp.mean(xv * xv, axis=-1, keepdims=True) + EPS)
        gg = dh * gain
        dx = inv * (gg - xv * (inv * inv * jnp.mean(gg * xv, axis=-1, keepdims=True)))
        dy[at_all, :] = (dy[at_all, :].astype(F32) + dx).astype(BF16)
        own[0:1, :] = own[0:1, :] + jnp.sum(dh * (xv * inv), axis=0, keepdims=True)

    store_dx = pltpu.make_async_copy(dy.at[mine, :], dx_out, loc_sem.at[1])
    store_dx.start()
    small.start(0)
    each(jobs_wo, 1, "mid")
    small.finish(0)
    small.start(1)
    each(jobs_wq, 0, "finish")
    each(jobs_wq, 1, "start")
    each(jobs_wo, 1, "finish")
    each(jobs_wo, 2, "start")
    small.finish(1)
    small.start(2)
    each(jobs_wq, 1, "mid")
    small.finish(2)
    small.start(3)
    each(jobs_wo, 2, "finish")
    each(jobs_wq, 1, "finish")
    each(jobs_wq, 2, "start")
    small.finish(3)
    both = ar[3, 0] + ar[3, 1]
    row = ar[3, tp]
    gain_out[...] = both[0]
    gbout_out[...] = both[1]
    bqkv_out[...] = row[2, 0:cols]
    lane = lax.broadcasted_iota(jnp.int32, (1, L), 1)
    sinks = jnp.zeros(lane.shape, F32)
    for n in range(width // L):
        sinks = jnp.where(lane == n, jnp.sum(row[3:4, n * L:n * L + L], axis=1, keepdims=True), sinks)
    sink_out[...] = sinks[0]
    each(jobs_wq, 2, "finish")
    copies.drain()
    store_y.wait()
    store_dx.wait()


VM = pl.BlockSpec(memory_space=pltpu.VMEM)
ANY = pl.BlockSpec(memory_space=pl.ANY)


def layer(wq, wo, x, x5, dy, small, perm, tab, base):
    half, d = x.shape
    cols, width = wq.shape[1], wo.shape[1]
    seq = 2 * half
    n = 11 + 10 + len(ORDERS) * 2 * 12 + len(WO_JOBS + WQ_JOBS) * 15
    sds = jax.ShapeDtypeStruct
    shapes = ((4, 4, 4) + wq.shape, (4, 4, 4) + wo.shape, (seq, d), (seq, d), (seq, cols), (seq, width), (d, cols), (width, d), (d, cols), (width, d), (half, width), (half, cols))
    scratch = [pltpu.VMEM(shape, BF16) for shape in shapes]
    scratch += [pltpu.VMEM((4, 4, 4, 24, cols), F32), pltpu.VMEM((4, 4, 48, d), F32), pltpu.VMEM((4, 4, 4, d), F32)]
    scratch += [pltpu.VMEM((2 * L, L), t) for t in (BF16, BF16, F32, F32)] + [pltpu.VMEM((1, width), F32)]
    scratch += [pltpu.SemaphoreType.DMA((k,)) for k in (3, n, n)]
    return pl.pallas_call(
        layer_kernel, name="layer",
        out_shape=(sds((half, d), BF16), sds((half, d), BF16), sds((24, cols), F32), sds((12, d), F32), sds((d,), F32), sds((d,), F32), sds((cols,), F32), sds((L,), F32)),
        in_specs=[VM, VM, ANY, ANY, ANY] + [VM] * 4, out_specs=(ANY, ANY) + (VM,) * 6, scratch_shapes=scratch + scatter_scratch(),
        compiler_params=pltpu.CompilerParams(collective_id=0, has_side_effects=True, vmem_limit_bytes=VMEM_LIMIT),
    )(wq, wo, x, x5, dy, small, perm, tab, base)


def rope_constants(n_blocks):
    freq = np.tile(ROPE_BASE ** (-2.0 * np.arange(L // 2) / L), 2)
    sign = np.where(np.arange(L) < L // 2, -1.0, 1.0)

    def pair(positions):
        angle = positions[:, None] * freq[None, :]
        return jnp.asarray(np.stack([np.cos(angle), np.sin(angle) * sign]), F32)

    return pair(np.arange(L)), pair(np.arange(n_blocks) * L)


def row_permutation():
    row = np.arange(96)[:, None]
    col = np.arange(192)[None, :]
    return jnp.asarray(np.stack([col == row // 12 * 24 + c * 12 + row % 12 for c in (0, 1)]), BF16)


def solution(mesh):
    act_spec = P("fsdp", "tp", None)
    wout_spec = P(("tp", "fsdp"), None)
    in_specs = (act_spec, act_spec, P(), P("fsdp", "tp"), P("tp"), P("tp"), wout_spec, P())
    out_specs = (act_spec, act_spec, P(), P("fsdp", "tp"), P("tp"), P("tp"), wout_spec, P())

    def device_step(resid_loc, grad_loc, norm_gain, wqkv_loc, bqkv_loc, sink_loc, wout_loc, b_out):
        x, dy = resid_loc[0], grad_loc[0]
        half, d = x.shape
        heads = sink_loc.shape[0]
        wo_slab = jnp.concatenate([wout_loc[:, :d // 2], wout_loc[:, d // 2:]], axis=0)
        rows = (norm_gain, b_out.astype(F32), bqkv_loc.astype(F32), jnp.repeat(sink_loc, L))
        small = jnp.stack([jnp.pad(r, (0, d - r.shape[0])) for r in rows])
        tab, base = rope_constants(2 * half // L)
        y, dx, gq, go, gain_g, bout_g, bqkv_g, sink_g = layer(wqkv_loc, wo_slab, x, x.reshape(2, 4, 4, 24, d), dy, small, row_permutation(), tab, base)
        return (y[None], dx[None], gain_g, gq, bqkv_g, sink_g[:heads], go, bout_g)

    return jax.shard_map(device_step, mesh=mesh, in_specs=in_specs, out_specs=out_specs, check_vma=False)
```

time: 195 us -> 145 us (0.74)
  local copies, waits for them, and re-layouts: 31.7 us -> 11.3 us
  Pallas kernels: 143 us -> 131 us
  matrix products: 11.5 us -> 0 us
  other arithmetic: 7.72 us -> 1.95 us
    pallas_call x3 -> x1, Pallas kernels: 143 us -> 131 us  [layer(): pl.pallas_call(layer_kernel, name='layer', out_shape=(sds((half, d), BF16...]
    dot_general x2 -> x0, matrix products: 11.5 us -> none  [the longest x1 6.37 us: device_step(): jnp.dot(h_all, wq, preferred_element_type=F32) + bqkv_loc.astype(F32)]
    transpose x2 -> x0, local copies, waits for them, and re-layouts: 8.33 us -> none  [wo_rows(): return w.reshape(64, 2, 12, d // 2).transpose(0, 2, 1, 3).reshape(width, d)]
    pallas_call x2 -> x0, local copies, waits for them, and re-layouts: 5.75 us -> none  [gather_all(): pl.pallas_call(gather_kernel, name='gather_all', out_shape=(wq_shape, wo_...]
    reshape x2 -> x1, local copies, waits for them, and re-layouts: 4.22 us -> 0.07 us  [device_step(): jnp.repeat(sink_loc, L)]
    neg x1 -> x0, other arithmetic: 2.81 us -> none  [rope_tables(): -sin]
    pallas_call x2 -> x0, other arithmetic: 2.62 us -> none  [all_grads(): pl.pallas_call(grads_kernel, name='all_grads', out_shape=(sds((half, d),...]
    unnamed x35 -> x24, local copies, waits for them, and re-layouts: 9.65 us -> 9.05 us
where the time goes in v2:
time: 145 us
  Pallas kernels  131 us (90%)
  local copies, waits for them, and re-layouts  11.3 us (8%)
  other arithmetic  1.95 us (1%)
    pallas_call x1, Pallas kernels, layer(): pl.pallas_call(layer_kernel, name='layer', out_shape=(sds((half, d), BF16...  131 us
    unnamed x24, local copies, waits for them, and re-layouts  9.05 us

profile of v2, /device:TPU:0, one launch (start us, length us, event | category | flops | bytes accessed | tf_op | source)
XLA Modules:
  0.0 145.1 jit_solution(17616066155655923876)
XLA Ops:
  0.6 0.0 copy-start
  0.6 0.6 copy-done
  1.3 0.1 broadcast_bitcast_fusion
  1.4 0.7 stack.21
  2.1 0.7 reshape.20
  2.8 0.7 pad_convert_fusion
  3.5 0.6 pad_maximum_fusion.1.small_in
  4.1 0.8 fusion
  4.9 0.6 pad_maximum_fusion.wo_in
  5.5 131.1 %layer.1 = (bf16[768,1536]{1,0:T(8,128)(2,1)}, bf16[768,1536]{1,0:T(8,128)(2,1)}, f32[24,1024]{1,0:T(8,128)}, f32[12,1536]{1,0:T(8,128)}, f32[1536]{0:T(1024)}, ...) custom-call(bf16[24,1024]{1,0:T(8,128)(2,1)} %wq_in.1, bf16[24,768]{1,0:T(8,128)(2,1)} %pad_maximum_fusion.wo_in, ...), custom_call_target="tpu_custom_call" | custom-call | tf_op jit(solution)/shard_map/layer/pallas_call | solution.py:598
  136.6 0.0 copy-start.1
  136.6 3.4 %copy.27 = bf16[1,768,1536]{2,1,0:T(8,128)(2,1)} copy(bf16[1,768,1536]{2,1,0:T(8,128)(2,1)} %bitcast.11) | data formatting | bytes 4718592
  140.0 0.0 copy-done.1
  140.0 0.0 copy-start.7
  140.0 0.0 copy-start.2
  140.1 0.0 copy-start.4
  140.1 1.4 copy.28
  141.5 0.6 copy.29
  142.1 0.0 copy-done.3
  142.1 0.6 copy.30
  142.7 0.6 copy.31
  143.3 0.5 copy.32
  143.8 0.6 copy.33
  144.5 0.6 copy.34
  (11 shorter events, 0.0 us)
Async XLA Ops:
  0.6 0.7 copy-start
  136.6 3.4 %copy-start.1 = (bf16[768,1536]{1,0:T(8,128)(2,1)S(1)}, bf16[768,1536]{1,0:T(8,128)(2,1)}, u32[]{:S(2)}) copy-start(bf16[768,1536]{1,0:T(8,128)(2,1)} %get-tuple-element.17) | copy-start | bytes 7077892
  140.0 1.4 copy-start.5
  140.0 2.1 %copy-start.3 = (f32[24,1024]{1,0:T(8,128)S(1)}, f32[24,1024]{1,0:T(8,128)}, u32[]{:S(2)}) copy-start(f32[24,1024]{1,0:T(8,128)} %get-tuple-element.37) | copy-start | bytes 294916
  140.0 2.7 %copy-start.6 = (f32[1024]{0:T(1024)S(1)}, f32[1024]{0:T(1024)}, u32[]{:S(2)}) copy-start(f32[1024]{0:T(1024)} %get-tuple-element.38) | copy-start | bytes 12292
  140.0 3.3 %copy-start.7 = (f32[128]{0:T(128)S(1)}, f32[128]{0:T(128)}, u32[]{:S(2)}) copy-start(f32[128]{0:T(128)} %get-tuple-element.21) | copy-start | bytes 1540
  140.0 3.8 %copy-start.2 = (f32[12,1536]{1,0:T(8,128)S(1)}, f32[12,1536]{1,0:T(8,128)}, u32[]{:S(2)}) copy-start(f32[12,1536]{1,0:T(8,128)} %get-tuple-element.40) | copy-start | bytes 221188
  140.1 4.4 %copy-start.4 = (f32[1536]{0:T(1024)S(1)}, f32[1536]{0:T(1024)}, u32[]{:S(2)}) copy-start(f32[1536]{0:T(1024)} %get-tuple-element.41) | copy-start | bytes 18436

commit v3 on v2

v3 whole, which is shorter than its diff:
```python
import math

import jax
import jax.numpy as jnp
import numpy as np
from jax import lax
from jax.experimental import pallas as pl
from jax.experimental.pallas import tpu as pltpu
from jax.sharding import PartitionSpec as P

EPS = 1e-5
ROPE_BASE = 150000.0
WINDOW = 128
MESH = pl.DeviceIdType.MESH
STRIDE = (16, 4, 1)
F32 = jnp.float32
BF16 = jnp.bfloat16
VMEM_LIMIT = 67_000_000
Z, Y, X = range(3)
UP, DOWN, FAR = 1, -1, 2
L = 128
PAIR = (0, 1)
RING = (4, 4)
NEG = -1e30


def coord(dim):
    return lax.rem(lax.div(lax.axis_index("fsdp"), STRIDE[dim]), 4)


def shifted(dim, k):
    return lax.rem(coord(dim) + (k + 4), 4)


def peer(dim, k):
    f = lax.axis_index("fsdp")
    return {"fsdp": f + (shifted(dim, k) - coord(dim)) * STRIDE[dim]}


def partner():
    return {"tp": 1 - lax.axis_index("tp")}


def span(n, size, base=0):
    return pl.ds(pl.multiple_of(base + n * size, math.gcd(size, L)), size)


def entry_barrier(peers):
    barrier = pltpu.get_barrier_semaphore()
    for p in peers:
        pl.semaphore_signal(barrier, inc=1, device_id=p, device_id_type=MESH)
    pl.semaphore_wait(barrier, len(peers))


class Copies:
    def __init__(self, send_sem, recv_sem):
        self.send_sem, self.recv_sem = send_sem, recv_sem
        self.n = 0
        self.sent = []

    def slots(self, count):
        first = self.n
        self.n += count
        return first

    def make(self, src, dst, slot, device):
        return pltpu.make_async_remote_copy(src_ref=src, dst_ref=dst, send_sem=self.send_sem.at[slot], recv_sem=self.recv_sem.at[slot], device_id=device, device_id_type=MESH)

    def send(self, src, dst, slot, device):
        copy = self.make(src, dst, slot, device)
        copy.start()
        self.sent.append(copy)

    def arrive(self, ref, slot, device):
        self.make(ref, ref, slot, device).wait_recv()

    def drain(self):
        for copy in self.sent:
            copy.wait_send()
        self.sent = []


class GatherStage:
    def __init__(self, copies, dim, slot_view, own_view):
        self.c, self.dim, self.view, self.own = copies, dim, slot_view, own_view
        self.base = copies.slots(6)

    def start(self):
        me = coord(self.dim)
        for h in PAIR:
            self.c.send(self.own(h), self.view(me, h), self.base + h, peer(self.dim, UP))
            self.c.send(self.own(1 - h), self.view(me, 1 - h), self.base + 3 - h, peer(self.dim, DOWN))

    def sides(self):
        return [(shifted(self.dim, k), peer(self.dim, k)) for k in (DOWN, UP)]

    def mid(self):
        (lo, down), (hi, up) = self.sides()
        self.c.arrive(self.view(lo, 0), self.base, down)
        self.c.send(self.view(lo, 0), self.view(lo, 0), self.base + 4, up)
        self.c.arrive(self.view(hi, 1), self.base + 3, up)
        self.c.send(self.view(hi, 1), self.view(hi, 1), self.base + 5, down)

    def finish(self):
        (lo, down), (hi, up) = self.sides()
        far = shifted(self.dim, FAR)
        for n, (at, h, dev) in enumerate(((lo, 1, down), (hi, 0, up))):
            self.c.arrive(self.view(at, h), self.base + 1 + n, dev)
            self.c.arrive(self.view(far, n), self.base + 4 + n, dev)


class GatherDirect:
    def __init__(self, copies, dim, view, own):
        self.c, self.dim, self.view, self.own = copies, dim, view, own
        self.base = copies.slots(3)

    def start(self):
        for slot, k in enumerate((UP, DOWN, FAR)):
            self.c.send(self.own(), self.view(coord(self.dim)), self.base + slot, peer(self.dim, k))

    def finish(self):
        for slot, k in enumerate((UP, DOWN, FAR)):
            self.c.arrive(self.view(shifted(self.dim, -k)), self.base + slot, peer(self.dim, k))


def gather_stages(copies, in_ref, out_ref, order, first, widths):
    whole = pl.ds(first, sum(widths))
    halves = [pl.ds(first, widths[0]), pl.ds(first + widths[0], widths[1])]

    def view(n, c, cols):
        idx = [coord(dim) for dim in (Z, Y, X)]
        for dim in order[:n]:
            idx[dim] = slice(None)
        idx[order[n]] = c
        return out_ref.at[tuple(idx) + (slice(None), cols)]

    return (GatherDirect(copies, order[0], lambda c: view(0, c, whole), lambda: in_ref.at[:, whole]),
            GatherDirect(copies, order[1], lambda c: view(1, c, whole), lambda: view(1, coord(order[1]), whole)),
            GatherStage(copies, order[2], lambda c, h: view(2, c, halves[h]), lambda h: view(2, coord(order[2]), halves[h])))


ORDERS = ((X, Y, Z), (Y, Z, X), (Z, X, Y))
WQ_GATHER = ((0, (256, L)), (384, (L, 256)), (768, (L, L)))
WO_GATHER = ((0, (L, L)), (256, (L, L)), (512, (L, L)))


def rotate(vals, cos, sin):
    return vals * cos + pltpu.roll(vals, L // 2, 1) * sin


def stack_heads(vals):
    return jnp.concatenate([vals[:, n:n + L] for n in range(0, vals.shape[1], L)], axis=0)


def unstack_heads(vals):
    return jnp.concatenate([vals[n:n + L, :] for n in range(0, vals.shape[0], L)], axis=1)


def dot_nn(a, b):
    return jnp.dot(a, b, preferred_element_type=F32)


def dot_tn(a, b):
    return lax.dot_general(a, b, (((0,), (0,)), ((), ())), preferred_element_type=F32)


def dot_nt(a, b):
    return lax.dot_general(a, b, (((1,), (1,)), ((), ())), preferred_element_type=F32)


class Attention:
    def __init__(self, qkv, o, d_o, tab, base, sink_ref, dsink, keys, vals, dk, dv, top, inv, bias):
        self.qkv, self.o, self.d_o, self.tab, self.base, self.dsink = qkv, o, d_o, tab, base, dsink
        self.keys, self.vals, self.dk, self.dv, self.top, self.inv, self.bias = keys, vals, dk, dv, top, inv, bias
        self.width = o.shape[1]
        self.blocks = o.shape[0] // L
        self.scale = L ** -0.5
        self.sink = jnp.concatenate([jnp.full((1, L), sink_ref[n], F32) for n in range(self.width // L)], axis=1)

    def prepare(self):
        for ref in (self.keys, self.vals, self.dk, self.dv):
            ref[pl.ds(0, L), :] = jnp.zeros((L, L), ref.dtype)
        self.dsink[...] = jnp.zeros(self.dsink.shape, F32)
        k_idx = lax.broadcasted_iota(jnp.int32, (2 * L, L), 0)
        q_idx = lax.broadcasted_iota(jnp.int32, (2 * L, L), 1)
        allowed = (k_idx > q_idx) & (k_idx <= q_idx + WINDOW)
        self.bias[1] = jnp.where(allowed, 0.0, NEG).astype(BF16)
        self.bias[0] = jnp.where(allowed & (k_idx >= WINDOW), 0.0, NEG).astype(BF16)

    def tables(self, i):
        cos_b, sin_b = self.base[0, pl.ds(i, 1), :], self.base[1, pl.ds(i, 1), :]
        cos_r, sin_r = self.tab[0], self.tab[1]
        return cos_b * cos_r - sin_b * sin_r, sin_b * cos_r + cos_b * sin_r

    def scores(self, i, keys, q, heads):
        bias = self.bias[jnp.minimum(i, 1)].astype(F32)
        return dot_nt(keys, q) * self.scale + jnp.concatenate([bias] * heads, axis=1)

    def forward(self, first, last):
        heads = self.width // L

        @pl.loop(first, last)
        def _(i):
            at, nxt = (span(i + n, L) for n in PAIR)
            cos, sin = self.tables(i)
            cos_all, sin_all = jnp.concatenate([cos] * heads, axis=0), jnp.concatenate([sin] * heads, axis=0)
            self.keys[nxt, :] = rotate(self.qkv[at, pl.ds(self.width, L)].astype(F32), cos, sin).astype(BF16)
            self.vals[nxt, :] = self.qkv[at, pl.ds(self.width + L, L)]
            for ref in (self.dk, self.dv):
                ref[nxt, :] = jnp.zeros((L, L), F32)
            q = rotate(stack_heads(self.qkv[at, pl.ds(0, self.width)]).astype(F32), cos_all, sin_all).astype(BF16)
            self.qkv[at, pl.ds(0, self.width)] = unstack_heads(q)
            pair = pl.ds(pl.multiple_of(i * L, L), 2 * L)
            scores = self.scores(i, self.keys[pair, :], q, heads)
            top = jnp.maximum(jnp.max(scores, axis=0, keepdims=True), self.sink)
            probs = jnp.exp(scores - top)
            inv = 1.0 / (jnp.sum(probs, axis=0, keepdims=True) + jnp.exp(self.sink - top))
            self.top[pl.ds(i, 1), :] = top
            self.inv[pl.ds(i, 1), :] = inv
            self.o[at, :] = unstack_heads(dot_tn((probs * inv).astype(BF16), self.vals[pair, :]).astype(BF16))

    def backward(self, g, first, last):
        heads = GROUP // L
        here = span(g, GROUP)
        sink = self.sink[:, g * GROUP:(g + 1) * GROUP]

        @pl.loop(first // TRIPLE, last // TRIPLE)
        def _(m):
            d_o = self.d_o[m, :, :, :, here].reshape(TRIPLE * L, GROUP)
            loads = []
            for n in range(TRIPLE):
                i = m * TRIPLE + n
                pair = pl.ds(pl.multiple_of(i * L, L), 2 * L)
                loads.append((i, stack_heads(self.qkv[span(i, L), here]), stack_heads(d_o[n * L:(n + 1) * L]), self.keys[pair, :], self.vals[pair, :],
                              self.top[pl.ds(i, 1), here], self.inv[pl.ds(i, 1), here], self.tables(i)))
            wide = [[jnp.concatenate([t] * heads, axis=0) for t in load[-1]] for load in loads]
            scores = [self.scores(i, keys, q, heads) for i, q, _, keys, *_ in loads]
            d_probs = [dot_nt(load[4], load[2]) for load in loads]
            probs = [jnp.exp(sc - load[5]) * load[6] for sc, load in zip(scores, loads)]
            d_probs = [dp.astype(BF16).astype(F32) for dp in d_probs]
            dvs = [dot_nn(p.astype(BF16), load[2]) for p, load in zip(probs, loads)]
            row_dots = [jnp.sum(p * dp, axis=0, keepdims=True) for p, dp in zip(probs, d_probs)]
            d_scores = [(p * (dp - rd)).astype(BF16) for p, dp, rd in zip(probs, d_probs, row_dots)]
            d_sink = self.dsink[:, here]
            for rd, load in zip(row_dots, loads):
                d_sink = d_sink - jnp.exp(sink - load[5]) * load[6] * rd
            dqs = [(dot_tn(ds, load[3]) * self.scale).astype(BF16).astype(F32) for ds, load in zip(d_scores, loads)]
            dks = [dot_nn(ds, load[1]) * self.scale for ds, load in zip(d_scores, loads)]
            stores = [unstack_heads(rotate(dq, cos, -sin).astype(BF16)) for dq, (cos, sin) in zip(dqs, wide)]
            self.dsink[:, here] = d_sink
            self.qkv[span(m, TRIPLE * L), here] = jnp.concatenate(stores, axis=0)
            rows = pl.ds(pl.multiple_of(m * TRIPLE * L, L), (TRIPLE + 1) * L)
            for ref, new in ((self.dv, dvs), (self.dk, dks)):
                parts = [new[0][:L]] + [p[L:] + q[:L] for p, q in zip(new, new[1:])] + [new[-1][L:]]
                ref[rows, :] = ref[rows, :] + jnp.concatenate(parts, axis=0)

    def backward_kv(self):
        @pl.loop(0, self.blocks)
        def _(i):
            at, nxt = (span(i + n, L) for n in PAIR)
            cos, sin = self.tables(i)
            self.qkv[at, pl.ds(self.width, L)] = rotate(self.dk[nxt, :].astype(BF16).astype(F32), cos, -sin).astype(BF16)
            self.qkv[at, pl.ds(self.width + L, L)] = self.dv[nxt, :].astype(BF16)


class ScatterStage:
    def __init__(self, copies, dim, blk, buf, put):
        self.c, self.dim, self.blk, self.buf, self.put = copies, dim, blk, buf, put
        self.base = copies.slots(6)
        self.a_up, self.a_down, self.lo = 0, 1, (2, 3)
        self.hi = (4, 5)

    def send(self, src, slot, k):
        self.c.send(src, self.buf.at[slot], self.base + slot, peer(self.dim, k))

    def arrive(self, slot, k):
        self.c.arrive(self.buf.at[slot], self.base + slot, peer(self.dim, k))

    def start(self):
        up, down, far = (shifted(self.dim, k) for k in (UP, DOWN, FAR))
        self.send(self.blk(far, 0), self.a_up, UP)
        self.send(self.blk(far, 1), self.a_down, DOWN)
        self.send(self.blk(up, 1), self.lo[1], UP)
        self.send(self.blk(down, 0), self.hi[0], DOWN)

    def add(self, slot, src):
        dst = self.buf.at[slot]
        if len(src.shape) == 2:
            dst[...] = dst[...] + src[...]
        else:
            @pl.loop(0, src.shape[0])
            def _(j):
                dst[j] = dst[j] + src[j]

    def mid(self):
        self.arrive(self.a_up, DOWN)
        self.add(self.a_up, self.blk(shifted(self.dim, UP), 0))
        self.arrive(self.a_down, UP)
        self.add(self.a_down, self.blk(shifted(self.dim, DOWN), 1))
        self.send(self.buf.at[self.a_up], self.lo[0], UP)
        self.send(self.buf.at[self.a_down], self.hi[1], DOWN)

    def finish(self):
        me = coord(self.dim)
        for h in (1, 0):
            self.arrive(self.lo[h], DOWN)
            self.arrive(self.hi[1 - h], UP)
        for h in PAIR:
            own, a, b = self.blk(me, h), self.buf.at[self.lo[h]], self.buf.at[self.hi[h]]
            if len(own.shape) == 2:
                self.put(h, None, own[...] + a[...] + b[...])
            else:
                @pl.loop(0, own.shape[0])
                def _(j):
                    self.put(h, j, own[j] + a[j] + b[j])


class DirectStage:
    def __init__(self, copies, dim, blk, buf, put):
        self.c, self.dim, self.blk, self.buf, self.put = copies, dim, blk, buf, put
        self.base = copies.slots(3)

    def start(self):
        for slot, k in enumerate((UP, DOWN, FAR)):
            self.c.send(self.blk(shifted(self.dim, k)), self.buf.at[slot], self.base + slot, peer(self.dim, k))

    def finish(self):
        for slot, k in enumerate((UP, DOWN, FAR)):
            self.c.arrive(self.buf.at[slot], self.base + slot, peer(self.dim, k))
        b = self.buf
        self.put((self.blk(coord(self.dim))[...] + b[0]) + (b[1] + b[2]))


def scatter_steps(copies, src, out, order, first, width, bufs, padded):
    r1, r2, r3, s2, s3 = bufs
    rows = out.shape[0]
    rest = [dim for dim in (Z, Y, X) if dim != order[0]]

    def pick(ref, at, t, h, cols):
        idx = [slice(None)] * (len(ref.shape) - 1)
        cut = 1 if at == 0 else 0
        half = ref.shape[cut] // 2
        idx[at], idx[cut] = t, pl.ds(h * half, half)
        return ref.at[tuple(idx) + (cols,)]

    def put1(h, j, val):
        s2[h * 2 + j] = val

    def put2(h, j, val):
        if padded:
            for t in PAIR:
                s3[h * 2 + t, 0:rows, :] = val[rows * t:rows * t + rows, :]
        else:
            s3[h * 2 + j] = val

    def put3(val):
        out[:, pl.ds(first, width)] = val[0:rows, :]

    one = ScatterStage(copies, order[0], lambda t, h: pick(src, order[0], t, h, pl.ds(first, width)), r1, put1)
    two = ScatterStage(copies, order[1], lambda t, h: pick(s2, rest.index(order[1]), t, h, slice(None)), r2, put2)
    three = DirectStage(copies, order[2], lambda t: s3.at[t], r3, put3)
    return iter(((one.start,), (one.mid,), (one.finish, two.start), (two.mid,), (two.finish, three.start), (three.finish,)))


def advance(*groups):
    for jobs in groups:
        for job in jobs:
            for step in next(job):
                step()


WO_JOBS = (((Y, Z, X), 0, 768), ((Z, Y, X), 768, 768))
GROUP = 2 * L
TRIPLE = 3
WQ_JOBS = tuple((order, first * L, size) for order, first, size in zip(ORDERS * 2, (0, 2, 3, 4, 6, 7), (GROUP, L, L) * 2))


def scatter_scratch():
    out = []
    for jobs, lead, rows, pad in ((WO_JOBS, (), 48, 16), (WQ_JOBS, (4,), 24, 24)):
        for _, _, width in jobs:
            half = (2, rows, width) if lead else (rows // 2, width)
            out += [pltpu.VMEM((6, 2) + lead + (rows, width), F32), pltpu.VMEM((6,) + half, F32), pltpu.VMEM((3, pad, width), F32),
                    pltpu.VMEM((4,) + lead + (rows, width), F32), pltpu.VMEM((4, pad, width), F32)]
    return out


class SmallSums:
    def __init__(self, copies, ar):
        self.c, self.ar = copies, ar
        self.base = copies.slots(10)

    def start(self, n):
        if n < 3:
            for slot, k in enumerate((UP, DOWN, FAR)):
                ref = self.ar.at[n, coord(n)]
                self.c.send(ref, ref, self.base + 3 * n + slot, peer(n, k))
        else:
            ref = self.ar.at[n, lax.axis_index("tp")]
            self.c.send(ref, ref, self.base + 3 * n, partner())

    def finish(self, n):
        ar = self.ar
        if n < 3:
            for slot, k in enumerate((UP, DOWN, FAR)):
                self.c.arrive(ar.at[n, shifted(n, -k)], self.base + 3 * n + slot, peer(n, k))
            total = (ar[n, 0] + ar[n, 1]) + (ar[n, 2] + ar[n, 3])
            ar[n + 1, coord(n + 1) if n < 2 else lax.axis_index("tp")] = total
        else:
            self.c.arrive(ar.at[n, 1 - lax.axis_index("tp")], self.base + 3 * n, partner())


def layer_kernel(wq_in, wo_in, x_in, x5_in, dy_in, gain_ref, bout_ref, bqkv_ref, sink_ref, perm_ref, tab_ref, base_ref,
                 y_out, dx_out, gq_out, go_out, gain_out, gbout_out, bqkv_out, sink_out, wo2_hbm, *scratch):
    bufs = list(scratch)
    (wq5, wo5, h, dy, qkv, o, wq, wo, wq2, o2, dqkv2, gq, go, ar, keys, vals, dk, dv, dsink, top, inv, bias, gain_sum,
     loc_sem, send_sem, recv_sem) = bufs[:26]
    bufs = bufs[26:]
    tp = lax.axis_index("tp")
    half, d = x_in.shape
    width, cols = o.shape[1], qkv.shape[1]
    start = tp * half
    mine, theirs = span(tp, half), span(1 - tp, half)
    wide, rest = pl.ds(0, cols), pl.ds(0, d - cols)
    x_low, x_high = qkv.at[pl.ds(0, half), :], qkv.at[pl.ds(half, half), rest]
    local = [pltpu.make_async_copy(a, b, loc_sem.at[n]) for n, (a, b) in enumerate((
        (x_in.at[:, wide], x_low), (x_in.at[:, pl.ds(cols, d - cols)], x_high), (dy_in, dy.at[mine, :])))]
    for copy in local:
        copy.start()
    for ref, own in ((wq5, wq_in), (wo5, wo_in)):
        ref[coord(Z), coord(Y), coord(X)] = own[...]
    entry_barrier([peer(dim, k) for dim in (Z, Y, X) for k in (UP, DOWN, FAR)] + [partner()])
    copies = Copies(send_sem, recv_sem)
    jobs_q = [gather_stages(copies, wq_in, wq5, order, *job) for order, job in zip(ORDERS, WQ_GATHER)]
    jobs_o = [gather_stages(copies, wo_in, wo5, order, *job) for order, job in zip(ORDERS, WO_GATHER)]

    def each(jobs, n, *names):
        for name in names:
            for job in jobs:
                getattr(job[n], name)()

    each(jobs_q, 0, "start")
    each(jobs_o, 0, "start")
    gain, b_out = gain_ref[...][None, :], bout_ref[...].astype(F32)[None, :]
    parts = 3
    step = half // parts
    slot_h = copies.slots(parts)
    slot_dy, slot_wq, slot_wo, slot_o, slot_dqkv = (copies.slots(n) for n in (1, 1, 1, 1, 3))
    att = Attention(qkv, o, wq5, tab_ref, base_ref, sink_ref, dsink, keys, vals, dk, dv, top, inv, bias)
    att.prepare()
    for copy in local:
        copy.wait()
    copies.send(dy.at[mine, :], dy.at[mine, :], slot_dy, partner())

    pieces = iter(range(parts))

    def norm_piece():
        k = next(pieces)
        first = k * step

        @pl.loop(0, step // 32)
        def _(i):
            at = span(i, 32, first)
            xv = jnp.concatenate([x_low[at, :], x_high[at, :]], axis=1).astype(F32)
            inv = lax.rsqrt(jnp.mean(xv * xv, axis=-1, keepdims=True) + EPS)
            h[span(i, 32, start + first), :] = (xv * inv * gain).astype(BF16)

        return k

    def send_piece(k):
        at = span(k, step, start)
        copies.send(h.at[at, :], h.at[at, :], slot_h + k, partner())

    ready = norm_piece()
    each(jobs_q, 0, "finish")
    each(jobs_q, 1, "start")
    each(jobs_o, 0, "finish")
    send_piece(ready)
    ready = norm_piece()
    each(jobs_q, 1, "finish")
    each(jobs_q, 2, "start")
    send_piece(ready)
    send_piece(norm_piece())
    each(jobs_q, 2, "mid")
    each(jobs_o, 1, "start")
    for k in range(parts):
        copies.arrive(h.at[span(k, step, (1 - tp) * half), :], slot_h + k, partner())
    copies.arrive(dy.at[theirs, :], slot_dy, partner())
    each(jobs_q, 2, "finish")

    @pl.loop(0, 16)
    def _(n):
        wq[span(n, 96), :] = wq5[lax.div(n, 4), lax.rem(n, 4)].reshape(96, cols)

    b_qkv = bqkv_ref[...].astype(F32)[None, :]
    tile = 384

    def qkv_tile(n):
        qkv[span(n, tile), :] = (dot_nn(h[span(n, tile), :], wq[...]) + b_qkv).astype(BF16)

    qkv_tile(0)
    copies.send(wq, wq2, slot_wq, partner())
    each(jobs_o, 1, "finish")
    each(jobs_o, 2, "start")
    for n in range(1, 4):
        qkv_tile(n)
    att.forward(0, att.blocks // 2)
    each(jobs_o, 2, "mid")
    att.forward(att.blocks // 2, att.blocks)
    copies.send(o.at[theirs, :], o2, slot_o, partner())
    each(jobs_o, 2, "finish")

    def slabs(z, pair):
        return wo5[z, pl.ds(pair * 2, 2)].reshape(192, d // 2)

    @pl.loop(0, 8)
    def _(n):
        group = slabs(lax.div(n, 2), lax.rem(n, 2))
        for c in PAIR:
            wo[span(n, 96), span(c, d // 2)] = dot_nn(perm_ref[c], group).astype(BF16)

    copies.send(wo, wo2_hbm, slot_wo, partner())
    scatters = []
    for jobs, src, out, padded in ((WO_JOBS, go, go_out, True), (WQ_JOBS, gq, gq_out, False)):
        for job in jobs:
            five, bufs = bufs[:5], bufs[5:]
            if padded:
                five[4][...] = jnp.zeros(five[4].shape, F32)
            scatters.append(scatter_steps(copies, src, out, *job, five, padded))
    s_wo, s_0, s_1, s_2 = scatters[:2], scatters[2:3], scatters[3:5], scatters[5:]

    @pl.loop(0, 2)
    def _(m):
        @pl.loop(0, 3)
        def _(n):
            at, to = span(m, tile), span(n, 2 * GROUP)
            go[pl.ds(m * 2, 2), :, :, to] = dot_tn(o[:, at], dy[:, to]).reshape(2, 4, 48, 2 * GROUP)

    copies.drain()
    advance(s_wo)
    @pl.loop(0, 4)
    def _(n):
        at = span(n, tile)
        wq5[n, :, :, :, pl.ds(0, width)] = dot_nt(dy[at, :], wo[...]).astype(BF16).reshape(*RING, 24, width)


    def done(g):
        return pl.ds(g * GROUP, GROUP if g < 2 else 2 * GROUP)

    def wq_grad(to):

        @pl.loop(0, 4)
        def _(m):
            gq[m, :, :, :, to] = dot_tn(h[:, span(m, tile)], qkv[:, to]).reshape(*RING, 24, to.size)

    early = 9
    plan = ((s_0, (s_wo,), ()), (s_1, (), (s_0,)), (s_2, (s_wo,), (s_0,)))
    for g, (jobs, during, after) in enumerate(plan):
        att.backward(g, 0, early)
        advance(*during)
        att.backward(g, early, att.blocks)
        if g == 2:
            att.backward_kv()
        copies.send(qkv.at[theirs, done(g)], dqkv2.at[:, done(g)], slot_dqkv + g, partner())
        if jobs is s_2:
            advance(s_1)
        wq_grad(done(g))
        advance(jobs)
        advance(*after)
    own = ar.at[Z, coord(Z)]
    own[...] = jnp.zeros(own.shape, F32)
    small = SmallSums(copies, ar)
    ones = jnp.ones((8, 2 * half), BF16)
    own[2:3, 0:cols] = dot_nn(ones, qkv[...])[0:1]
    own[3:4, 0:width] = dsink[...]
    own[1:2, :] = dot_nn(ones[:, 0:half], dy[mine, :])[0:1]
    loads = [pltpu.make_async_copy(x5_in.at[:, :, :, :, span(c, d // 2)], wo5.at[pl.ds(c * 2, 2)], loc_sem.at[c]) for c in PAIR]
    wo2 = h.at[pl.ds(0, half), :]
    loads.append(pltpu.make_async_copy(wo2_hbm, wo2, loc_sem.at[2]))
    for ref, slot in ((wo2_hbm, slot_wo), (wq2, slot_wq), (o2, slot_o)):
        copies.arrive(ref, slot, partner())
    for copy in loads:
        copy.start()
    for g in range(3):
        copies.arrive(dqkv2.at[:, done(g)], slot_dqkv + g, partner())
    wide_half = d // 2

    def dh_tiles(c):
        to = span(c, wide_half)

        @pl.loop(0, 2)
        def _(n):
            h[span(n, tile, half), to] = (dot_nt(qkv[span(n, tile, start), :], wq[to, :]) + dot_nt(dqkv2[span(n, tile), :], wq2[to, :])).astype(BF16)

    dh_tiles(0)
    advance(s_wo, s_0)
    dh_tiles(1)
    for copy in loads:
        copy.wait()
    advance(s_1, s_2)
    rows = 48
    gain_sum[...] = jnp.zeros(gain_sum.shape, F32)

    def norm_back(c):
        count = half // rows // 2

        @pl.loop(c * count, c * count + count)
        def _(n):
            at = span(n, rows, start)
            z, yy, pair = lax.div(n, 8), lax.rem(lax.div(n, 2), 4), pl.ds(lax.rem(n, 2) * 2, 2)
            xv = jnp.concatenate([wo5[z + c, yy, pair].reshape(rows, d // 2) for c in (0, 2)], axis=1).astype(F32)
            dh = h[span(n, rows, half), :].astype(F32)
            inv = lax.rsqrt(jnp.mean(xv * xv, axis=-1, keepdims=True) + EPS)
            xn, gg = xv * inv, dh * gain
            dx = inv * (gg - xn * jnp.mean(gg * xn, axis=-1, keepdims=True))
            dy[at, :] = (dy[at, :].astype(F32) + dx).astype(BF16)
            gain_sum[...] = gain_sum[...] + jnp.sum((dh * xn).reshape(rows // 8, 8, d), axis=0)

    norm_back(0)
    advance(s_wo, s_0, s_1)
    norm_back(1)
    own[0:1, :] = jnp.sum(gain_sum[...], axis=0, keepdims=True)
    store_dx = pltpu.make_async_copy(dy.at[mine, :], dx_out, loc_sem.at[1])
    store_dx.start()
    small.start(0)
    advance(s_0, s_2)
    def y_tiles(c):
        to = span(c, wide_half)

        @pl.loop(0, 2)
        def _(n):
            at = span(n, tile)
            xv = wo5[n + 2 * c].reshape(tile, wide_half).astype(F32)
            acc = dot_nn(o[span(n, tile, start), :], wo[:, to]) + dot_nn(o2[at, :], wo2[:, to])
            dy[span(n, tile, (1 - tp) * half), to] = (xv + acc + b_out[:, c * wide_half:(c + 1) * wide_half]).astype(BF16)

    y_tiles(0)
    small.finish(0)
    small.start(1)
    advance(s_1)
    y_tiles(1)
    store_y = pltpu.make_async_copy(dy.at[theirs, :], y_out, loc_sem.at[0])
    store_y.start()
    small.finish(1)
    small.start(2)
    advance(s_2)
    small.finish(2)
    small.start(3)
    advance(s_wo, s_1)
    advance(s_2)
    small.finish(3)
    advance(s_2)
    both = ar[3, 0] + ar[3, 1]
    row = ar[3, tp]
    gain_out[...] = both[0]
    gbout_out[...] = both[1]
    bqkv_out[...] = row[2, 0:cols]
    lane = lax.broadcasted_iota(jnp.int32, (1, L), 1)
    sinks = jnp.zeros(lane.shape, F32)
    for n in range(width // L):
        sinks = jnp.where(lane == n, jnp.sum(row[3:4, n * L:n * L + L], axis=1, keepdims=True), sinks)
    sink_out[...] = sinks[0]
    for jobs in (s_wo, s_0, s_1, s_2):
        for job in jobs:
            assert next(job, None) is None
    copies.drain()
    store_y.wait()
    store_dx.wait()


VM = pl.BlockSpec(memory_space=pltpu.VMEM)
ANY = pl.BlockSpec(memory_space=pl.ANY)


def layer(wq, wo, x, x5, dy, gain, b_out, b_qkv, sinks, perm, tab, base):
    half, d = x.shape
    cols, width = wq.shape[1], wo.shape[1]
    seq = 2 * half
    n = 10 + 10 + len(ORDERS) * 2 * 12 + len(WO_JOBS + WQ_JOBS) * 15
    sds = jax.ShapeDtypeStruct
    shapes = ((4,) + RING + wq.shape, (4,) + RING + wo.shape, (seq, d), (seq, d), (seq, cols), (seq, width), (d, cols), (width, d), (d, cols), (half, width), (half, cols))
    scratch = [pltpu.VMEM(shape, BF16) for shape in shapes]
    scratch += [pltpu.VMEM((4, *RING, 24, cols), F32), pltpu.VMEM((*RING, 48, d), F32), pltpu.VMEM((4, *RING, d), F32)]
    scratch += [pltpu.VMEM((seq + L, L), t) for t in (BF16, BF16, F32, F32)] + [pltpu.VMEM((1, width), F32)]
    scratch += [pltpu.VMEM((seq // L, width), F32)] * 2 + [pltpu.VMEM((2, 2 * L, L), BF16), pltpu.VMEM((8, d), F32)]
    scratch += [pltpu.SemaphoreType.DMA((k,)) for k in (3, n, n)]
    outs = (sds((half, d), BF16), sds((half, d), BF16), sds((24, cols), F32), sds((12, d), F32), sds((d,), F32), sds((d,), F32), sds((cols,), F32), sds((L,), F32))
    results = pl.pallas_call(
        layer_kernel, name="layer", out_shape=outs + (sds((width, d), BF16),),
        in_specs=[VM, VM, ANY, ANY, ANY, VM, VM, VM, pl.BlockSpec(memory_space=pltpu.SMEM)] + [VM] * 3, out_specs=(ANY, ANY) + (VM,) * 6 + (ANY,), scratch_shapes=scratch + scatter_scratch(),
        compiler_params=pltpu.CompilerParams(collective_id=0, has_side_effects=True, vmem_limit_bytes=VMEM_LIMIT),
    )(wq, wo, x, x5, dy, gain, b_out, b_qkv, sinks, perm, tab, base)
    return pl.pallas_call(
        hand_over, name="hand_over", out_shape=outs, in_specs=[ANY, ANY] + [VM] * 6, out_specs=(ANY, ANY) + (VM,) * 6,
        scratch_shapes=[pltpu.VMEM((2, half, d), BF16), pltpu.SemaphoreType.DMA((2, 3)), pltpu.SemaphoreType.DMA((2, 3))],
    )(*results[:-1])


def hand_over(*refs):
    ins, outs = refs[:8], refs[8:16]
    buf, in_sem, out_sem = refs[16:]
    parts = in_sem.shape[1]
    step = buf.shape[1] // parts
    copies = []
    for n in range(parts):
        at = pl.ds(n * step, step)
        for c in PAIR:
            copies.append((pltpu.make_async_copy(ins[c].at[at, :], buf.at[c, at, :], in_sem.at[c, n]), pltpu.make_async_copy(buf.at[c, at, :], outs[c].at[at, :], out_sem.at[c, n])))
    for load, _ in copies:
        load.start()
    for a, b in zip(ins[2:], outs[2:]):
        b[...] = a[...]
    for load, store in copies:
        load.wait()
        store.start()
    for _, store in copies:
        store.wait()


def rope_constants(n_blocks):
    freq = np.tile(ROPE_BASE ** (-2.0 * np.arange(L // 2) / L), 2)
    sign = np.where(np.arange(L) < L // 2, -1.0, 1.0)

    def pair(positions):
        angle = positions[:, None] * freq[None, :]
        return jnp.asarray(np.stack([np.cos(angle), np.sin(angle) * sign]), F32)

    return pair(np.arange(L)), pair(np.arange(n_blocks) * L)


def row_permutation():
    row = np.arange(96)[:, None]
    col = np.arange(192)[None, :]
    return jnp.asarray(np.stack([col == row // 12 * 24 + c * 12 + row % 12 for c in PAIR]), BF16)


def solution(mesh):
    act_spec = P("fsdp", "tp", None)
    wout_spec = P(("tp", "fsdp"), None)
    in_specs = (act_spec, act_spec, P(), P("fsdp", "tp"), P("tp"), P("tp"), wout_spec, P())
    out_specs = (act_spec, act_spec, P(), P("fsdp", "tp"), P("tp"), P("tp"), wout_spec, P())

    def device_step(resid_loc, grad_loc, norm_gain, wqkv_loc, bqkv_loc, sink_loc, wout_loc, b_out):
        x, dy = resid_loc[0], grad_loc[0]
        half, d = x.shape
        heads = sink_loc.shape[0]
        wo_slab = jnp.concatenate([wout_loc[:, :d // 2], wout_loc[:, d // 2:]], axis=0)
        tab, base = rope_constants(2 * half // L)
        y, dx, gq, go, gain_g, bout_g, bqkv_g, sink_g = layer(wqkv_loc, wo_slab, x, x.reshape(2, *RING, 24, d), dy, norm_gain, b_out, bqkv_loc, sink_loc, row_permutation(), tab, base)
        return (y[None], dx[None], gain_g, gq, bqkv_g, sink_g[:heads], go, bout_g)

    return jax.shard_map(device_step, mesh=mesh, in_specs=in_specs, out_specs=out_specs, check_vma=False)
```

time: 145 us -> 124 us (0.86)
  local copies, waits for them, and re-layouts: 11.3 us -> 0.76 us
  Pallas kernels: 131 us -> 121 us
    pallas_call x1 -> x2, Pallas kernels: 131 us -> 121 us  [the longest x1 116 us: layer(): pl.pallas_call(layer_kernel, name='layer', out_shape=outs + (sds((width,...]
    unnamed x24 -> x0, local copies, waits for them, and re-layouts: 9.05 us -> none
where the time goes in v3:
time: 124 us; the launch traced here: 123 us
  Pallas kernels  121 us (98%)
    pallas_call x1, Pallas kernels, layer(): pl.pallas_call(layer_kernel, name='layer', out_shape=outs + (sds((width,...  116 us
    pallas_call x1, Pallas kernels, layer(): pl.pallas_call(hand_over, name='hand_over', out_shape=outs, in_specs=[ANY...  5.62 us

profile of v3, /device:TPU:0, one launch (start us, length us, event | category | flops | bytes accessed | tf_op | source)
XLA Modules:
  0.0 123.3 jit_solution(6963218664578551792)
XLA Ops:
  0.6 0.8 fusion
  1.4 0.6 pad_maximum_fusion.wo_in
  2.0 115.5 %layer.1 = (bf16[768,1536]{1,0:T(8,128)(2,1)}, bf16[768,1536]{1,0:T(8,128)(2,1)}, f32[24,1024]{1,0:T(8,128)}, f32[12,1536]{1,0:T(8,128)}, f32[1536]{0:T(1024)}, ...) custom-call(bf16[24,1024]{1,0:T(8,128)(2,1)} %wq_in.1, ...), custom_call_target="tpu_custom_call" | custom-call | tf_op jit(solution)/shard_map/layer/pallas_call | solution.py:688
  117.5 5.6 %hand_over.1 = (bf16[768,1536]{1,0:T(8,128)(2,1)}, bf16[768,1536]{1,0:T(8,128)(2,1)}, f32[24,1024]{1,0:T(8,128)}, f32[12,1536]{1,0:T(8,128)}, f32[1536]{0:T(1024...) custom-call(bf16[768,1536]{1,0:T(8,128)(2,1)} %get-tuple-element.24.refs_0_, ...), custom_call_target="tpu_custom_call" | custom-call | tf_op jit(solution)/shard_map/hand_over/pallas_call | solution.py:693

commit v4 on v3

--- a/solution.py
+++ b/solution.py
@@ -21,6 +21,8 @@
 L = 128
 PAIR = (0, 1)
 RING = (4, 4)
+GROUP = 2 * L
+TRIPLE = 3
 NEG = -1e30
 
 
@@ -64,11 +66,13 @@
         return first
 
     def make(self, src, dst, slot, device):
-        return pltpu.make_async_remote_copy(src_ref=src, dst_ref=dst, send_sem=self.send_sem.at[slot], recv_sem=self.recv_sem.at[slot], device_id=device, device_id_type=MESH)
+        send = len(self.sent) % self.send_sem.shape[0]
+        return pltpu.make_async_remote_copy(src_ref=src, dst_ref=dst, send_sem=self.send_sem.at[send], recv_sem=self.recv_sem.at[slot], device_id=device, device_id_type=MESH)
 
     def send(self, src, dst, slot, device):
         copy = self.make(src, dst, slot, device)
         copy.start()
+        assert len(self.sent) < self.send_sem.shape[0]
         self.sent.append(copy)
 
     def arrive(self, ref, slot, device):
@@ -123,25 +127,25 @@
             self.c.arrive(self.view(shifted(self.dim, -k)), self.base + slot, peer(self.dim, k))
 
 
-def gather_stages(copies, in_ref, out_ref, order, first, widths):
-    whole = pl.ds(first, sum(widths))
-    halves = [pl.ds(first, widths[0]), pl.ds(first + widths[0], widths[1])]
-
-    def view(n, c, cols):
+def gather_stages(copies, in_ref, out_ref, order, first, size):
+    rows = pl.ds(first, size)
+
+    def view(n, c, h=None):
         idx = [coord(dim) for dim in (Z, Y, X)]
         for dim in order[:n]:
             idx[dim] = slice(None)
         idx[order[n]] = c
-        return out_ref.at[tuple(idx) + (slice(None), cols)]
-
-    return (GatherDirect(copies, order[0], lambda c: view(0, c, whole), lambda: in_ref.at[:, whole]),
-            GatherDirect(copies, order[1], lambda c: view(1, c, whole), lambda: view(1, coord(order[1]), whole)),
-            GatherStage(copies, order[2], lambda c, h: view(2, c, halves[h]), lambda h: view(2, coord(order[2]), halves[h])))
+        if h is not None:
+            cut = min(order[:n])
+            idx[cut] = pl.ds(h * 2, 2)
+        return out_ref.at[tuple(idx) + (rows,)]
+
+    return (GatherDirect(copies, order[0], lambda c: view(0, c), lambda: in_ref.at[rows]),
+            GatherDirect(copies, order[1], lambda c: view(1, c), lambda: view(1, coord(order[1]))),
+            GatherStage(copies, order[2], lambda c, h: view(2, c, h), lambda h: view(2, coord(order[2]), h)))
 
 
 ORDERS = ((X, Y, Z), (Y, Z, X), (Z, X, Y))
-WQ_GATHER = ((0, (256, L)), (384, (L, 256)), (768, (L, L)))
-WO_GATHER = ((0, (L, L)), (256, (L, L)), (512, (L, L)))
 
 
 def rotate(vals, cos, sin):
@@ -181,8 +185,8 @@
         for ref in (self.keys, self.vals, self.dk, self.dv):
             ref[pl.ds(0, L), :] = jnp.zeros((L, L), ref.dtype)
         self.dsink[...] = jnp.zeros(self.dsink.shape, F32)
-        k_idx = lax.broadcasted_iota(jnp.int32, (2 * L, L), 0)
-        q_idx = lax.broadcasted_iota(jnp.int32, (2 * L, L), 1)
+        k_idx = lax.broadcasted_iota(jnp.int32, (GROUP, L), 0)
+        q_idx = lax.broadcasted_iota(jnp.int32, (GROUP, L), 1)
         allowed = (k_idx > q_idx) & (k_idx <= q_idx + WINDOW)
         self.bias[1] = jnp.where(allowed, 0.0, NEG).astype(BF16)
         self.bias[0] = jnp.where(allowed & (k_idx >= WINDOW), 0.0, NEG).astype(BF16)
@@ -199,25 +203,33 @@
     def forward(self, first, last):
         heads = self.width // L
 
-        @pl.loop(first, last)
-        def _(i):
-            at, nxt = (span(i + n, L) for n in PAIR)
-            cos, sin = self.tables(i)
-            cos_all, sin_all = jnp.concatenate([cos] * heads, axis=0), jnp.concatenate([sin] * heads, axis=0)
-            self.keys[nxt, :] = rotate(self.qkv[at, pl.ds(self.width, L)].astype(F32), cos, sin).astype(BF16)
-            self.vals[nxt, :] = self.qkv[at, pl.ds(self.width + L, L)]
+        @pl.loop(first // len(PAIR), last // len(PAIR))
+        def _(m):
+            at = span(m, GROUP)
+            blocks = [m * len(PAIR) + n for n in PAIR]
+            tables = [self.tables(i) for i in blocks]
+            cos, sin = (jnp.concatenate(t, axis=0) for t in zip(*tables))
+            new = pl.ds(pl.multiple_of(m * GROUP + L, L), GROUP)
+            self.keys[new, :] = rotate(self.qkv[at, pl.ds(self.width, L)].astype(F32), cos, sin).astype(BF16)
+            self.vals[new, :] = self.qkv[at, pl.ds(self.width + L, L)]
             for ref in (self.dk, self.dv):
-                ref[nxt, :] = jnp.zeros((L, L), F32)
-            q = rotate(stack_heads(self.qkv[at, pl.ds(0, self.width)]).astype(F32), cos_all, sin_all).astype(BF16)
-            self.qkv[at, pl.ds(0, self.width)] = unstack_heads(q)
-            pair = pl.ds(pl.multiple_of(i * L, L), 2 * L)
-            scores = self.scores(i, self.keys[pair, :], q, heads)
-            top = jnp.maximum(jnp.max(scores, axis=0, keepdims=True), self.sink)
-            probs = jnp.exp(scores - top)
-            inv = 1.0 / (jnp.sum(probs, axis=0, keepdims=True) + jnp.exp(self.sink - top))
-            self.top[pl.ds(i, 1), :] = top
-            self.inv[pl.ds(i, 1), :] = inv
-            self.o[at, :] = unstack_heads(dot_tn((probs * inv).astype(BF16), self.vals[pair, :]).astype(BF16))
+                ref[new, :] = jnp.zeros((GROUP, L), F32)
+            seen = pl.ds(pl.multiple_of(m * GROUP, L), TRIPLE * L)
+            all_keys, all_vals = self.keys[seen, :], self.vals[seen, :]
+            keys, vals = ([t[n * L:n * L + GROUP] for n in PAIR] for t in (all_keys, all_vals))
+            raw = [stack_heads(self.qkv[span(i, L), pl.ds(0, self.width)]) for i in blocks]
+            wide = [[jnp.concatenate([t] * heads, axis=0) for t in pair] for pair in tables]
+            queries = [rotate(q.astype(F32), *w).astype(BF16) for q, w in zip(raw, wide)]
+            scores = [self.scores(i, k, q, heads) for i, k, q in zip(blocks, keys, queries)]
+            tops = [jnp.maximum(jnp.max(sc, axis=0, keepdims=True), self.sink) for sc in scores]
+            probs = [jnp.exp(sc - top) for sc, top in zip(scores, tops)]
+            invs = [1.0 / (jnp.sum(p, axis=0, keepdims=True) + jnp.exp(self.sink - top)) for p, top in zip(probs, tops)]
+            outs = [dot_tn((p * inv).astype(BF16), v) for p, inv, v in zip(probs, invs, vals)]
+            for ref, parts in ((self.o, outs), (self.qkv, queries)):
+                ref[at, pl.ds(0, self.width)] = jnp.concatenate([unstack_heads(p.astype(BF16)) for p in parts], axis=0)
+            for i, top, inv in zip(blocks, tops, invs):
+                self.top[pl.ds(i, 1), :] = top
+                self.inv[pl.ds(i, 1), :] = inv
 
     def backward(self, g, first, last):
         heads = GROUP // L
@@ -230,7 +242,7 @@
             loads = []
             for n in range(TRIPLE):
                 i = m * TRIPLE + n
-                pair = pl.ds(pl.multiple_of(i * L, L), 2 * L)
+                pair = pl.ds(pl.multiple_of(i * L, L), GROUP)
                 loads.append((i, stack_heads(self.qkv[span(i, L), here]), stack_heads(d_o[n * L:(n + 1) * L]), self.keys[pair, :], self.vals[pair, :],
                               self.top[pl.ds(i, 1), here], self.inv[pl.ds(i, 1), here], self.tables(i)))
             wide = [[jnp.concatenate([t] * heads, axis=0) for t in load[-1]] for load in loads]
@@ -347,19 +359,23 @@
         s2[h * 2 + j] = val
 
     def put2(h, j, val):
-        if padded:
-            for t in PAIR:
-                s3[h * 2 + t, 0:rows, :] = val[rows * t:rows * t + rows, :]
-        else:
-            s3[h * 2 + j] = val
+        for t in PAIR:
+            s3[h * 2 + t, 0:rows, :] = val[rows * t:rows * t + rows, :]
+
+    def put_slabs(val):
+        s3[...] = val
 
     def put3(val):
         out[:, pl.ds(first, width)] = val[0:rows, :]
 
     one = ScatterStage(copies, order[0], lambda t, h: pick(src, order[0], t, h, pl.ds(first, width)), r1, put1)
-    two = ScatterStage(copies, order[1], lambda t, h: pick(s2, rest.index(order[1]), t, h, slice(None)), r2, put2)
     three = DirectStage(copies, order[2], lambda t: s3.at[t], r3, put3)
-    return iter(((one.start,), (one.mid,), (one.finish, two.start), (two.mid,), (two.finish, three.start), (three.finish,)))
+    if padded:
+        two = ScatterStage(copies, order[1], lambda t, h: pick(s2, rest.index(order[1]), t, h, slice(None)), r2, put2)
+        return iter(((one.start,), (one.mid,), (one.finish, two.start), (two.mid,), (two.finish, three.start), (three.finish,)))
+    side = rest.index(order[1])
+    two = DirectStage(copies, order[1], lambda t: s2.at[(slice(None),) * side + (t,)], r2, put_slabs)
+    return iter(((one.start,), (one.mid,), (one.finish, two.start), (two.finish, three.start), (three.finish,)))
 
 
 def advance(*groups):
@@ -370,8 +386,6 @@
 
 
 WO_JOBS = (((Y, Z, X), 0, 768), ((Z, Y, X), 768, 768))
-GROUP = 2 * L
-TRIPLE = 3
 WQ_JOBS = tuple((order, first * L, size) for order, first, size in zip(ORDERS * 2, (0, 2, 3, 4, 6, 7), (GROUP, L, L) * 2))
 
 
@@ -379,8 +393,8 @@
     out = []
     for jobs, lead, rows, pad in ((WO_JOBS, (), 48, 16), (WQ_JOBS, (4,), 24, 24)):
         for _, _, width in jobs:
-            half = (2, rows, width) if lead else (rows // 2, width)
-            out += [pltpu.VMEM((6, 2) + lead + (rows, width), F32), pltpu.VMEM((6,) + half, F32), pltpu.VMEM((3, pad, width), F32),
+            second = (3, 4, rows, width) if lead else (6, rows // 2, width)
+            out += [pltpu.VMEM((6, 2) + lead + (rows, width), F32), pltpu.VMEM(second, F32), pltpu.VMEM((3, pad, width), F32),
                     pltpu.VMEM((4,) + lead + (rows, width), F32), pltpu.VMEM((4, pad, width), F32)]
     return out
 
@@ -411,11 +425,11 @@
 
 
 def layer_kernel(wq_in, wo_in, x_in, x5_in, dy_in, gain_ref, bout_ref, bqkv_ref, sink_ref, perm_ref, tab_ref, base_ref,
-                 y_out, dx_out, gq_out, go_out, gain_out, gbout_out, bqkv_out, sink_out, wo2_hbm, *scratch):
-    bufs = list(scratch)
+                 y_out, dx_out, *outs_and_scratch):
+    hbm_outs, wo2_hbm, bufs = outs_and_scratch[:6], outs_and_scratch[6], list(outs_and_scratch[7:])
     (wq5, wo5, h, dy, qkv, o, wq, wo, wq2, o2, dqkv2, gq, go, ar, keys, vals, dk, dv, dsink, top, inv, bias, gain_sum,
-     loc_sem, send_sem, recv_sem) = bufs[:26]
-    bufs = bufs[26:]
+     gq_out, go_out, gain_out, gbout_out, bqkv_out, sink_out, loc_sem, send_sem, recv_sem) = bufs[:32]
+    bufs = bufs[32:]
     tp = lax.axis_index("tp")
     half, d = x_in.shape
     width, cols = o.shape[1], qkv.shape[1]
@@ -431,8 +445,7 @@
         ref[coord(Z), coord(Y), coord(X)] = own[...]
     entry_barrier([peer(dim, k) for dim in (Z, Y, X) for k in (UP, DOWN, FAR)] + [partner()])
     copies = Copies(send_sem, recv_sem)
-    jobs_q = [gather_stages(copies, wq_in, wq5, order, *job) for order, job in zip(ORDERS, WQ_GATHER)]
-    jobs_o = [gather_stages(copies, wo_in, wo5, order, *job) for order, job in zip(ORDERS, WO_GATHER)]
+    jobs_q, jobs_o = ([gather_stages(copies, a, b, order, 8 * n, 8) for n, order in enumerate(ORDERS)] for a, b in ((wq_in, wq5), (wo_in, wo5)))
 
     def each(jobs, n, *names):
         for name in names:
@@ -565,8 +578,7 @@
         if jobs is s_2:
             advance(s_1)
         wq_grad(done(g))
-        advance(jobs)
-        advance(*after)
+        advance(*after, jobs)
     own = ar.at[Z, coord(Z)]
     own[...] = jnp.zeros(own.shape, F32)
     small = SmallSums(copies, ar)
@@ -593,11 +605,11 @@
             h[span(n, tile, half), to] = (dot_nt(qkv[span(n, tile, start), :], wq[to, :]) + dot_nt(dqkv2[span(n, tile), :], wq2[to, :])).astype(BF16)
 
     dh_tiles(0)
-    advance(s_wo, s_0)
+    advance(s_wo)
     dh_tiles(1)
     for copy in loads:
         copy.wait()
-    advance(s_1, s_2)
+    advance(s_1, s_0, s_2)
     rows = 48
     gain_sum[...] = jnp.zeros(gain_sum.shape, F32)
 
@@ -617,13 +629,13 @@
             gain_sum[...] = gain_sum[...] + jnp.sum((dh * xn).reshape(rows // 8, 8, d), axis=0)
 
     norm_back(0)
-    advance(s_wo, s_0, s_1)
+    advance(s_wo)
     norm_back(1)
     own[0:1, :] = jnp.sum(gain_sum[...], axis=0, keepdims=True)
-    store_dx = pltpu.make_async_copy(dy.at[mine, :], dx_out, loc_sem.at[1])
+    store_dx = pltpu.make_async_copy(dy.at[mine, :], dx_out, loc_sem.at[7])
     store_dx.start()
     small.start(0)
-    advance(s_0, s_2)
+    advance(s_0, s_1)
     def y_tiles(c):
         to = span(c, wide_half)
 
@@ -637,17 +649,16 @@
     y_tiles(0)
     small.finish(0)
     small.start(1)
-    advance(s_1)
+    advance(s_2)
     y_tiles(1)
-    store_y = pltpu.make_async_copy(dy.at[theirs, :], y_out, loc_sem.at[0])
+    store_y = pltpu.make_async_copy(dy.at[theirs, :], y_out, loc_sem.at[6])
     store_y.start()
     small.finish(1)
     small.start(2)
-    advance(s_2)
+    advance(s_2, s_1)
     small.finish(2)
     small.start(3)
-    advance(s_wo, s_1)
-    advance(s_2)
+    advance(s_wo)
     small.finish(3)
     advance(s_2)
     both = ar[3, 0] + ar[3, 1]
@@ -660,12 +671,16 @@
     for n in range(width // L):
         sinks = jnp.where(lane == n, jnp.sum(row[3:4, n * L:n * L + L], axis=1, keepdims=True), sinks)
     sink_out[...] = sinks[0]
+    stores = [pltpu.make_async_copy(a, b, loc_sem.at[n]) for n, (a, b) in enumerate(zip((gq_out, go_out, gain_out, gbout_out, bqkv_out, sink_out), hbm_outs))]
+    for copy in stores[1:]:
+        copy.start()
     for jobs in (s_wo, s_0, s_1, s_2):
         for job in jobs:
             assert next(job, None) is None
     copies.drain()
-    store_y.wait()
-    store_dx.wait()
+    stores[0].start()
+    for copy in stores + [store_y, store_dx]:
+        copy.wait()
 
 
 VM = pl.BlockSpec(memory_space=pltpu.VMEM)
@@ -676,40 +691,38 @@
     half, d = x.shape
     cols, width = wq.shape[1], wo.shape[1]
     seq = 2 * half
-    n = 10 + 10 + len(ORDERS) * 2 * 12 + len(WO_JOBS + WQ_JOBS) * 15
+    n = 10 + 10 + len(ORDERS + ORDERS + WQ_JOBS) * 12 + len(WO_JOBS) * 15
     sds = jax.ShapeDtypeStruct
     shapes = ((4,) + RING + wq.shape, (4,) + RING + wo.shape, (seq, d), (seq, d), (seq, cols), (seq, width), (d, cols), (width, d), (d, cols), (half, width), (half, cols))
     scratch = [pltpu.VMEM(shape, BF16) for shape in shapes]
     scratch += [pltpu.VMEM((4, *RING, 24, cols), F32), pltpu.VMEM((*RING, 48, d), F32), pltpu.VMEM((4, *RING, d), F32)]
     scratch += [pltpu.VMEM((seq + L, L), t) for t in (BF16, BF16, F32, F32)] + [pltpu.VMEM((1, width), F32)]
-    scratch += [pltpu.VMEM((seq // L, width), F32)] * 2 + [pltpu.VMEM((2, 2 * L, L), BF16), pltpu.VMEM((8, d), F32)]
-    scratch += [pltpu.SemaphoreType.DMA((k,)) for k in (3, n, n)]
+    scratch += [pltpu.VMEM((seq // L, width), F32)] * 2 + [pltpu.VMEM((2, GROUP, L), BF16), pltpu.VMEM((8, d), F32)]
     outs = (sds((half, d), BF16), sds((half, d), BF16), sds((24, cols), F32), sds((12, d), F32), sds((d,), F32), sds((d,), F32), sds((cols,), F32), sds((L,), F32))
+    scratch += [pltpu.VMEM(o.shape, F32) for o in outs[2:]] + [pltpu.SemaphoreType.DMA((k,)) for k in (8, n * 3 // 5, n)]
     results = pl.pallas_call(
         layer_kernel, name="layer", out_shape=outs + (sds((width, d), BF16),),
-        in_specs=[VM, VM, ANY, ANY, ANY, VM, VM, VM, pl.BlockSpec(memory_space=pltpu.SMEM)] + [VM] * 3, out_specs=(ANY, ANY) + (VM,) * 6 + (ANY,), scratch_shapes=scratch + scatter_scratch(),
+        in_specs=[VM, VM, ANY, ANY, ANY, VM, VM, VM, pl.BlockSpec(memory_space=pltpu.SMEM)] + [VM] * 3, out_specs=(ANY,) * 9, scratch_shapes=scratch + scatter_scratch(),
         compiler_params=pltpu.CompilerParams(collective_id=0, has_side_effects=True, vmem_limit_bytes=VMEM_LIMIT),
     )(wq, wo, x, x5, dy, gain, b_out, b_qkv, sinks, perm, tab, base)
     return pl.pallas_call(
-        hand_over, name="hand_over", out_shape=outs, in_specs=[ANY, ANY] + [VM] * 6, out_specs=(ANY, ANY) + (VM,) * 6,
-        scratch_shapes=[pltpu.VMEM((2, half, d), BF16), pltpu.SemaphoreType.DMA((2, 3)), pltpu.SemaphoreType.DMA((2, 3))],
+        hand_over, name="hand_over", out_shape=outs, in_specs=[ANY] * 8, out_specs=(ANY,) * 8,
+        scratch_shapes=[pltpu.VMEM(o.shape, o.dtype) for o in outs] + [pltpu.SemaphoreType.DMA((8, 4))] * 2,
     )(*results[:-1])
 
 
 def hand_over(*refs):
-    ins, outs = refs[:8], refs[8:16]
-    buf, in_sem, out_sem = refs[16:]
-    parts = in_sem.shape[1]
-    step = buf.shape[1] // parts
+    ins, outs, bufs = refs[:8], refs[8:16], refs[16:24]
+    in_sem, out_sem = refs[24:]
     copies = []
-    for n in range(parts):
-        at = pl.ds(n * step, step)
-        for c in PAIR:
-            copies.append((pltpu.make_async_copy(ins[c].at[at, :], buf.at[c, at, :], in_sem.at[c, n]), pltpu.make_async_copy(buf.at[c, at, :], outs[c].at[at, :], out_sem.at[c, n])))
+    for k, (a, buf, b) in enumerate(zip(ins, bufs, outs)):
+        parts = in_sem.shape[1] if k < 2 else 1
+        step = a.shape[0] // parts
+        for n in range(parts):
+            at = pl.ds(n * step, step)
+            copies.append((pltpu.make_async_copy(a.at[at], buf.at[at], in_sem.at[k, n]), pltpu.make_async_copy(buf.at[at], b.at[at], out_sem.at[k, n])))
     for load, _ in copies:
         load.start()
-    for a, b in zip(ins[2:], outs[2:]):
-        b[...] = a[...]
     for load, store in copies:
         load.wait()
         store.start()

time: 124 us -> 113 us (0.911)
  Pallas kernels: 121 us -> 111 us
    pallas_call x1, Pallas kernels: 116 us -> 106 us  [layer(): pl.pallas_call(layer_kernel, name='layer', out_shape=outs + (sds((width,...]
where the time goes in v4:
time: 113 us
  Pallas kernels  111 us (98%)
    pallas_call x1, Pallas kernels, layer(): pl.pallas_call(layer_kernel, name='layer', out_shape=outs + (sds((width,...  106 us
    pallas_call x1, Pallas kernels, layer(): pl.pallas_call(hand_over, name='hand_over', out_shape=outs, in_specs=[ANY...  4.61 us

profile of v4, /device:TPU:0, one launch (start us, length us, event | category | flops | bytes accessed | tf_op | source)
XLA Modules:
  0.0 112.7 jit_solution(7407366111389485214)
XLA Ops:
  0.6 0.8 fusion
  1.4 0.6 pad_maximum_fusion.wo_in
  2.0 105.9 %layer.1 = (bf16[768,1536]{1,0:T(8,128)(2,1)}, bf16[768,1536]{1,0:T(8,128)(2,1)}, f32[24,1024]{1,0:T(8,128)}, f32[12,1536]{1,0:T(8,128)}, f32[1536]{0:T(1024)}, ...) custom-call(bf16[24,1024]{1,0:T(8,128)(2,1)} %wq_in.1, ...), custom_call_target="tpu_custom_call" | custom-call | tf_op jit(solution)/shard_map/layer/pallas_call | solution.py:703
  107.9 4.6 %hand_over.1 = (bf16[768,1536]{1,0:T(8,128)(2,1)}, bf16[768,1536]{1,0:T(8,128)(2,1)}, f32[24,1024]{1,0:T(8,128)}, f32[12,1536]{1,0:T(8,128)}, f32[1536]{0:T(1024...) custom-call(bf16[768,1536]{1,0:T(8,128)(2,1)} %get-tuple-element.24.refs_0_, ...), custom_call_target="tpu_custom_call" | custom-call | tf_op jit(solution)/shard_map/hand_over/pallas_call | solution.py:708

commit v5 on v4

--- a/solution.py
+++ b/solution.py
@@ -231,12 +231,12 @@
                 self.top[pl.ds(i, 1), :] = top
                 self.inv[pl.ds(i, 1), :] = inv
 
-    def backward(self, g, first, last):
+    def backward(self, g):
         heads = GROUP // L
         here = span(g, GROUP)
         sink = self.sink[:, g * GROUP:(g + 1) * GROUP]
 
-        @pl.loop(first // TRIPLE, last // TRIPLE)
+        @pl.loop(0, self.blocks // TRIPLE)
         def _(m):
             d_o = self.d_o[m, :, :, :, here].reshape(TRIPLE * L, GROUP)
             loads = []
@@ -343,13 +343,13 @@
         self.put((self.blk(coord(self.dim))[...] + b[0]) + (b[1] + b[2]))
 
 
-def scatter_steps(copies, src, out, order, first, width, bufs, padded):
+def scatter_steps(copies, src, out, order, first, width, band, bufs, padded):
     r1, r2, r3, s2, s3 = bufs
-    rows = out.shape[0]
+    rows = out.shape[0] if padded else band.size
     rest = [dim for dim in (Z, Y, X) if dim != order[0]]
 
-    def pick(ref, at, t, h, cols):
-        idx = [slice(None)] * (len(ref.shape) - 1)
+    def pick(ref, at, t, h, in_band, cols):
+        idx = [slice(None)] * (len(ref.shape) - 2) + [in_band]
         cut = 1 if at == 0 else 0
         half = ref.shape[cut] // 2
         idx[at], idx[cut] = t, pl.ds(h * half, half)
@@ -366,12 +366,12 @@
         s3[...] = val
 
     def put3(val):
-        out[:, pl.ds(first, width)] = val[0:rows, :]
-
-    one = ScatterStage(copies, order[0], lambda t, h: pick(src, order[0], t, h, pl.ds(first, width)), r1, put1)
+        out[pl.ds(0, rows) if padded else band, pl.ds(first, width)] = val[0:rows, :]
+
+    one = ScatterStage(copies, order[0], lambda t, h: pick(src, order[0], t, h, band, pl.ds(first, width)), r1, put1)
     three = DirectStage(copies, order[2], lambda t: s3.at[t], r3, put3)
     if padded:
-        two = ScatterStage(copies, order[1], lambda t, h: pick(s2, rest.index(order[1]), t, h, slice(None)), r2, put2)
+        two = ScatterStage(copies, order[1], lambda t, h: pick(s2, rest.index(order[1]), t, h, slice(None), slice(None)), r2, put2)
         return iter(((one.start,), (one.mid,), (one.finish, two.start), (two.mid,), (two.finish, three.start), (three.finish,)))
     side = rest.index(order[1])
     two = DirectStage(copies, order[1], lambda t: s2.at[(slice(None),) * side + (t,)], r2, put_slabs)
@@ -385,17 +385,19 @@
                 step()
 
 
-WO_JOBS = (((Y, Z, X), 0, 768), ((Z, Y, X), 768, 768))
-WQ_JOBS = tuple((order, first * L, size) for order, first, size in zip(ORDERS * 2, (0, 2, 3, 4, 6, 7), (GROUP, L, L) * 2))
+WO_JOBS = tuple((order, n * 768, 768, pl.ds(0, 48)) for n, order in enumerate(((Y, Z, X), (Z, Y, X))))
+SLAB = pl.ds(0, 24)
+WQ_JOBS = tuple((order, first * L, size, SLAB) for order, first, size in zip(ORDERS * 2, (0, 2, 3, 4, 6, 7), (GROUP, L, L) * 2))
 
 
 def scatter_scratch():
     out = []
-    for jobs, lead, rows, pad in ((WO_JOBS, (), 48, 16), (WQ_JOBS, (4,), 24, 24)):
-        for _, _, width in jobs:
+    for jobs, lead, pad in ((WO_JOBS, (), 16), (WQ_JOBS, (4,), None)):
+        for _, _, width, band in jobs:
+            rows = band.size
             second = (3, 4, rows, width) if lead else (6, rows // 2, width)
-            out += [pltpu.VMEM((6, 2) + lead + (rows, width), F32), pltpu.VMEM(second, F32), pltpu.VMEM((3, pad, width), F32),
-                    pltpu.VMEM((4,) + lead + (rows, width), F32), pltpu.VMEM((4, pad, width), F32)]
+            shapes = ((6, 2) + lead + (rows, width), second, (3, pad or rows, width), (4,) + lead + (rows, width), (4, pad or rows, width))
+            out += [pltpu.VMEM(shape, F32) for shape in shapes]
     return out
 
 
@@ -566,19 +568,15 @@
         def _(m):
             gq[m, :, :, :, to] = dot_tn(h[:, span(m, tile)], qkv[:, to]).reshape(*RING, 24, to.size)
 
-    early = 9
-    plan = ((s_0, (s_wo,), ()), (s_1, (), (s_0,)), (s_2, (s_wo,), (s_0,)))
-    for g, (jobs, during, after) in enumerate(plan):
-        att.backward(g, 0, early)
-        advance(*during)
-        att.backward(g, early, att.blocks)
+    for g, (jobs, after) in enumerate(((s_0, s_wo), (s_1, s_0), (s_2, s_wo + s_0))):
+        att.backward(g)
         if g == 2:
             att.backward_kv()
         copies.send(qkv.at[theirs, done(g)], dqkv2.at[:, done(g)], slot_dqkv + g, partner())
         if jobs is s_2:
             advance(s_1)
         wq_grad(done(g))
-        advance(*after, jobs)
+        advance(after, jobs)
     own = ar.at[Z, coord(Z)]
     own[...] = jnp.zeros(own.shape, F32)
     small = SmallSums(copies, ar)
@@ -609,7 +607,6 @@
     dh_tiles(1)
     for copy in loads:
         copy.wait()
-    advance(s_1, s_0, s_2)
     rows = 48
     gain_sum[...] = jnp.zeros(gain_sum.shape, F32)
 
@@ -629,13 +626,13 @@
             gain_sum[...] = gain_sum[...] + jnp.sum((dh * xn).reshape(rows // 8, 8, d), axis=0)
 
     norm_back(0)
-    advance(s_wo)
+    advance(s_2)
     norm_back(1)
     own[0:1, :] = jnp.sum(gain_sum[...], axis=0, keepdims=True)
     store_dx = pltpu.make_async_copy(dy.at[mine, :], dx_out, loc_sem.at[7])
     store_dx.start()
     small.start(0)
-    advance(s_0, s_1)
+    advance(s_1)
     def y_tiles(c):
         to = span(c, wide_half)
 
@@ -649,7 +646,7 @@
     y_tiles(0)
     small.finish(0)
     small.start(1)
-    advance(s_2)
+    advance(s_2, s_0, s_wo)
     y_tiles(1)
     store_y = pltpu.make_async_copy(dy.at[theirs, :], y_out, loc_sem.at[6])
     store_y.start()
@@ -658,9 +655,8 @@
     advance(s_2, s_1)
     small.finish(2)
     small.start(3)
-    advance(s_wo)
+    advance(s_0, s_wo, s_1, s_2)
     small.finish(3)
-    advance(s_2)
     both = ar[3, 0] + ar[3, 1]
     row = ar[3, tp]
     gain_out[...] = both[0]
@@ -712,8 +708,9 @@
 
 
 def hand_over(*refs):
-    ins, outs, bufs = refs[:8], refs[8:16], refs[16:24]
-    in_sem, out_sem = refs[24:]
+    *refs, in_sem, out_sem = refs
+    n = len(refs) // 3
+    ins, outs, bufs = refs[:n], refs[n:2 * n], refs[2 * n:]
     copies = []
     for k, (a, buf, b) in enumerate(zip(ins, bufs, outs)):
         parts = in_sem.shape[1] if k < 2 else 1

time: 113 us -> 112 us (level)
  Pallas kernels: 111 us -> 109 us
    pallas_call x1, Pallas kernels: 106 us -> 105 us  [layer(): pl.pallas_call(layer_kernel, name='layer', out_shape=outs + (sds((width,...]
where the time goes in v5:
time: 112 us
  Pallas kernels  109 us (97%)
    pallas_call x1, Pallas kernels, layer(): pl.pallas_call(layer_kernel, name='layer', out_shape=outs + (sds((width,...  105 us
    pallas_call x1, Pallas kernels, layer(): pl.pallas_call(hand_over, name='hand_over', out_shape=outs, in_specs=[ANY...  4.61 us

profile of v5, /device:TPU:0, one launch (start us, length us, event | category | flops | bytes accessed | tf_op | source)
XLA Modules:
  0.0 111.5 jit_solution(4257443732729185833)
XLA Ops:
  0.6 0.8 fusion
  1.4 0.6 pad_maximum_fusion.wo_in
  2.0 104.7 %layer.1 = (bf16[768,1536]{1,0:T(8,128)(2,1)}, bf16[768,1536]{1,0:T(8,128)(2,1)}, f32[24,1024]{1,0:T(8,128)}, f32[12,1536]{1,0:T(8,128)}, f32[1536]{0:T(1024)}, ...) custom-call(bf16[24,1024]{1,0:T(8,128)(2,1)} %wq_in.1, ...), custom_call_target="tpu_custom_call" | custom-call | tf_op jit(solution)/shard_map/layer/pallas_call | solution.py:699
  106.8 4.6 %hand_over.1 = (bf16[768,1536]{1,0:T(8,128)(2,1)}, bf16[768,1536]{1,0:T(8,128)(2,1)}, f32[24,1024]{1,0:T(8,128)}, f32[12,1536]{1,0:T(8,128)}, f32[1536]{0:T(1024...) custom-call(bf16[768,1536]{1,0:T(8,128)(2,1)} %get-tuple-element.24.refs_0_, ...), custom_call_target="tpu_custom_call" | custom-call | tf_op jit(solution)/shard_map/hand_over/pallas_call | solution.py:704

commit v6 on v5

--- a/solution.py
+++ b/solution.py
@@ -278,12 +278,12 @@
 class ScatterStage:
     def __init__(self, copies, dim, blk, buf, put):
         self.c, self.dim, self.blk, self.buf, self.put = copies, dim, blk, buf, put
-        self.base = copies.slots(6)
+        self.base = copies.slots(3)
         self.a_up, self.a_down, self.lo = 0, 1, (2, 3)
         self.hi = (4, 5)
 
     def send(self, src, slot, k):
-        self.c.send(src, self.buf.at[slot], self.base + slot, peer(self.dim, k))
+        self.c.send(src, self.buf.at[slot], self.base + min(slot, 2), peer(self.dim, k))
 
     def arrive(self, slot, k):
         self.c.arrive(self.buf.at[slot], self.base + slot, peer(self.dim, k))
@@ -314,9 +314,7 @@
 
     def finish(self):
         me = coord(self.dim)
-        for h in (1, 0):
-            self.arrive(self.lo[h], DOWN)
-            self.arrive(self.hi[1 - h], UP)
+        self.c.arrive(self.buf.at[pl.ds(2, 4)], self.base + 2, peer(self.dim, UP))
         for h in PAIR:
             own, a, b = self.blk(me, h), self.buf.at[self.lo[h]], self.buf.at[self.hi[h]]
             if len(own.shape) == 2:
@@ -330,15 +328,14 @@
 class DirectStage:
     def __init__(self, copies, dim, blk, buf, put):
         self.c, self.dim, self.blk, self.buf, self.put = copies, dim, blk, buf, put
-        self.base = copies.slots(3)
+        self.base = copies.slots(1)
 
     def start(self):
         for slot, k in enumerate((UP, DOWN, FAR)):
-            self.c.send(self.blk(shifted(self.dim, k)), self.buf.at[slot], self.base + slot, peer(self.dim, k))
+            self.c.send(self.blk(shifted(self.dim, k)), self.buf.at[slot], self.base, peer(self.dim, k))
 
     def finish(self):
-        for slot, k in enumerate((UP, DOWN, FAR)):
-            self.c.arrive(self.buf.at[slot], self.base + slot, peer(self.dim, k))
+        self.c.arrive(self.buf, self.base, peer(self.dim, UP))
         b = self.buf
         self.put((self.blk(coord(self.dim))[...] + b[0]) + (b[1] + b[2]))
 
@@ -687,7 +684,7 @@
     half, d = x.shape
     cols, width = wq.shape[1], wo.shape[1]
     seq = 2 * half
-    n = 10 + 10 + len(ORDERS + ORDERS + WQ_JOBS) * 12 + len(WO_JOBS) * 15
+    n = 10 + 10 + len(ORDERS + ORDERS) * 12 + len(WQ_JOBS) * 5 + len(WO_JOBS) * 7
     sds = jax.ShapeDtypeStruct
     shapes = ((4,) + RING + wq.shape, (4,) + RING + wo.shape, (seq, d), (seq, d), (seq, cols), (seq, width), (d, cols), (width, d), (d, cols), (half, width), (half, cols))
     scratch = [pltpu.VMEM(shape, BF16) for shape in shapes]
@@ -695,7 +692,7 @@
     scratch += [pltpu.VMEM((seq + L, L), t) for t in (BF16, BF16, F32, F32)] + [pltpu.VMEM((1, width), F32)]
     scratch += [pltpu.VMEM((seq // L, width), F32)] * 2 + [pltpu.VMEM((2, GROUP, L), BF16), pltpu.VMEM((8, d), F32)]
     outs = (sds((half, d), BF16), sds((half, d), BF16), sds((24, cols), F32), sds((12, d), F32), sds((d,), F32), sds((d,), F32), sds((cols,), F32), sds((L,), F32))
-    scratch += [pltpu.VMEM(o.shape, F32) for o in outs[2:]] + [pltpu.SemaphoreType.DMA((k,)) for k in (8, n * 3 // 5, n)]
+    scratch += [pltpu.VMEM(o.shape, F32) for o in outs[2:]] + [pltpu.SemaphoreType.DMA((k,)) for k in (8, 116, n)]
     results = pl.pallas_call(
         layer_kernel, name="layer", out_shape=outs + (sds((width, d), BF16),),
         in_specs=[VM, VM, ANY, ANY, ANY, VM, VM, VM, pl.BlockSpec(memory_space=pltpu.SMEM)] + [VM] * 3, out_specs=(ANY,) * 9, scratch_shapes=scratch + scatter_scratch(),

time: 112 us -> 111 us (level)
  no operation moved by 1% of the time
where the time goes in v6:
time: 111 us
  Pallas kernels  109 us (98%)
    pallas_call x1, Pallas kernels, layer(): pl.pallas_call(layer_kernel, name='layer', out_shape=outs + (sds((width,...  104 us
    pallas_call x1, Pallas kernels, layer(): pl.pallas_call(hand_over, name='hand_over', out_shape=outs, in_specs=[ANY...  4.61 us

profile of v6, /device:TPU:0, one launch (start us, length us, event | category | flops | bytes accessed | tf_op | source)
XLA Modules:
  0.0 111.0 jit_solution(16108418769386673298)
XLA Ops:
  0.6 0.8 fusion
  1.4 0.6 pad_maximum_fusion.wo_in
  2.0 104.2 %layer.1 = (bf16[768,1536]{1,0:T(8,128)(2,1)}, bf16[768,1536]{1,0:T(8,128)(2,1)}, f32[24,1024]{1,0:T(8,128)}, f32[12,1536]{1,0:T(8,128)}, f32[1536]{0:T(1024)}, ...) custom-call(bf16[24,1024]{1,0:T(8,128)(2,1)} %wq_in.1, ...), custom_call_target="tpu_custom_call" | custom-call | tf_op jit(solution)/shard_map/layer/pallas_call | solution.py:696
  106.2 4.6 %hand_over.1 = (bf16[768,1536]{1,0:T(8,128)(2,1)}, bf16[768,1536]{1,0:T(8,128)(2,1)}, f32[24,1024]{1,0:T(8,128)}, f32[12,1536]{1,0:T(8,128)}, f32[1536]{0:T(1024...) custom-call(bf16[768,1536]{1,0:T(8,128)(2,1)} %get-tuple-element.24.refs_0_, ...), custom_call_target="tpu_custom_call" | custom-call | tf_op jit(solution)/shard_map/hand_over/pallas_call | solution.py:701
